TPU v7x, 32 devices: a whole 2x2x4 slice. The times are simulated.
32 devices in a mesh: doc: 2 (over x), seq: 4 (over y, core), head: 4 (over z).
Axes of the slice: x: 2, y: 2, z: 4, core: 2. Of those that a mesh axis runs over, the one named last changes fastest.
Arguments:
- length: int32 [2], P('doc'), parts along dimension 0, may hold values from 896 to 1024
- residual: bfloat16 [2048, 4096], P(('doc', 'seq'), 'head'), parts along dimension 0, may hold values from -6 to 6
- ssm_input: bfloat16 [2048, 4096], P(('doc', 'seq'), 'head'), parts along dimension 0, may hold values from -6 to 6
- state_in: bfloat16 [2048, 128], P(('doc', 'seq')), parts along dimension 0, may hold values from -6 to 6
- state_out: bfloat16 [2048, 128], P(('doc', 'seq')), parts along dimension 0, may hold values from -0.5 to 0.5
- step_raw: float32 [128, 1024], P(('doc', 'head'), 'seq'), parts along dimension 0, may hold values from -5 to 2
- decay_rate: float32 [64], P('head'), may hold values from 0 to 1, as said below
- ssm_gain: float32 [4096], P('head'), may hold values from 0.1 to 1.9
- out_weight: bfloat16 [4096, 4096], P('head'), may hold values from -0.09375 to 0.09375
- norm_gain: float32 [4096], replicated, may hold values from 0.1 to 1.9
- query_weight: bfloat16 [4096, 4096], P(None, 'head'), may hold values from -2 to 2
- key_weight: bfloat16 [4096, 1024], P(None, 'head'), may hold values from -3 to 3
- value_weight: bfloat16 [4096, 1024], P(None, 'head'), may hold values from -0.09375 to 0.09375
Outputs:
- layer_out: bfloat16 [2048, 4096], P(('doc', 'seq'), 'head'), parts along dimension 0
- head_out: bfloat16 [2048, 4096], P(('doc', 'seq'), 'head'), parts along dimension 0
There are 2 independent parts, one for each index of `doc`. A program takes and returns all parts, laid end to end along the dimension named above; an argument that names none is the same for every part. Nothing has to cross between parts.
Inputs may be any that keep to these rules, and one draw needn't show every extreme that they name: The document fills positions 0 to length - 1 of the 1024; later positions are padding. `decay_rate`: positive.
All inputs are finite; a program needn't handle non-finite values.
Results may differ from a plain program's by a relative error of at most 0.028.
The roundings to bfloat16 on the way count: a program that leaves them out, or rounds other values in their place, can miss the bound.
Values may be sent and summed in bfloat16 or wider, within the bound.
A program may use at most 64 MiB of HBM per device.

v0:
```python
import jax
import jax.numpy as jnp
from jax import lax
from jax.sharding import PartitionSpec as P

HEAD_DIM = 128


EPSILON = 1e-05
NEG_BIG = -1e30
HIGHEST = lax.Precision.HIGHEST


def prefix_2(value, axis, join, neutral):
    count, mine = (lax.axis_size(axis), lax.axis_index(axis))
    pieces = jax.tree.map(lambda part: lax.all_gather(part, axis), value)
    so_far = jax.tree.map(
        lambda part, zero: jnp.full_like(part, 0) + jnp.asarray(zero, part.dtype), value, neutral
    )

    def turn(position, so_far):
        longer = join(so_far, jax.tree.map(lambda part: part[position], pieces))
        return jax.tree.map(lambda new, old: jnp.where(position < mine, new, old), longer, so_far)

    return lax.fori_loop(0, count - 1, turn, so_far)


def chain_link(earlier, later):
    return (earlier[0] * later[0], later[0][:, None, None] * earlier[1] + later[1])


def body(
    length,
    residual,
    ssm_input,
    state_in,
    state_out,
    step_raw,
    decay_rate,
    ssm_gain,
    out_weight,
    norm_gain,
    query_weight,
    key_weight,
    value_weight,
):
    rows = residual.shape[0]
    local_heads = decay_rate.shape[0]
    head_width = ssm_input.shape[1] // local_heads
    seq_index = lax.axis_index("seq")
    limit = length[0]
    positions = seq_index * rows + jnp.arange(rows, dtype=jnp.int32)
    live_rows = positions < limit
    live = live_rows.astype(jnp.float32)
    delta = live[None, :] * jax.nn.softplus(step_raw)
    cumlog = jnp.cumsum(-decay_rate[:, None] * delta, axis=1)
    inputs = ssm_input.astype(jnp.float32).reshape(rows, local_heads, head_width)
    inner = jnp.dot(state_out, state_in.T, preferred_element_type=jnp.float32)
    causal = jnp.arange(rows)[:, None] >= jnp.arange(rows)[None, :]
    spread = cumlog[:, :, None] - cumlog[:, None, :]
    mixing = (
        jnp.where(causal[None], jnp.exp(jnp.where(causal[None], spread, 0.0)), 0.0)
        * inner[None]
        * delta[:, None, :]
    )
    within = jnp.einsum("hts,shp->thp", mixing, inputs, precision=HIGHEST)
    tail = jnp.exp(cumlog[:, -1:] - cumlog) * delta
    local_state = jnp.einsum(
        "hs,shp,sn->hpn", tail, inputs, state_in.astype(jnp.float32), precision=HIGHEST
    )
    block_decay = jnp.exp(cumlog[:, -1])
    prefix = prefix_2(
        (block_decay, local_state),
        "seq",
        chain_link,
        (jnp.ones_like(block_decay), jnp.zeros_like(local_state)),
    )
    incoming = prefix[1]
    carried = jnp.einsum("hpn,tn->thp", incoming, state_out.astype(jnp.float32), precision=HIGHEST)
    ssm_out = (within + jnp.exp(cumlog).T[:, :, None] * carried) * live[:, None, None]
    mean_square = jnp.mean(ssm_out * ssm_out, axis=2, keepdims=True)
    normed = (
        ssm_out * lax.rsqrt(mean_square + EPSILON) * ssm_gain.reshape(local_heads, head_width)
    ).astype(jnp.bfloat16)
    normed = normed.reshape(rows, local_heads * head_width)
    partial_value = jnp.dot(normed, out_weight, preferred_element_type=jnp.float32)
    model_width = norm_gain.shape[0]
    own_width = residual.shape[1]
    projected = lax.psum_scatter(partial_value, "head", scatter_dimension=1, tiled=True)
    layer_out = (residual.astype(jnp.float32) + projected).astype(jnp.bfloat16)
    widened = layer_out.astype(jnp.float32)
    squares = lax.psum(jnp.sum(widened * widened, axis=1), "head")
    piece_gain = lax.dynamic_slice_in_dim(norm_gain, lax.axis_index("head") * own_width, own_width)
    scaled = (widened * lax.rsqrt(squares / model_width + EPSILON)[:, None] * piece_gain).astype(
        jnp.bfloat16
    )
    attn_in = lax.all_gather(scaled, "head", axis=1, tiled=True)
    queries = jnp.dot(attn_in, query_weight, preferred_element_type=jnp.float32).astype(
        jnp.bfloat16
    )
    keys = jnp.dot(attn_in, key_weight, preferred_element_type=jnp.float32).astype(jnp.bfloat16)
    values = jnp.dot(attn_in, value_weight, preferred_element_type=jnp.float32).astype(jnp.bfloat16)
    query_local = query_weight.shape[1] // HEAD_DIM
    kv_local = key_weight.shape[1] // HEAD_DIM
    group_size = query_local // kv_local
    grouped = queries.reshape(rows, kv_local, group_size, HEAD_DIM)
    best = jnp.full((rows, query_local), NEG_BIG, jnp.float32)
    key_piece = lax.all_gather(keys, "seq", axis=0, tiled=True)
    value_piece = lax.all_gather(values, "seq", axis=0, tiled=True)
    count = key_piece.shape[0]
    key_pos = jnp.arange(count, dtype=jnp.int32)
    allowed = (key_pos[None, :] <= positions[:, None]) & (key_pos[None, :] < limit)
    scores = jnp.einsum(
        "tkgd,rkd->tkgr",
        grouped,
        key_piece.reshape(count, kv_local, HEAD_DIM),
        preferred_element_type=jnp.float32,
    ) * HEAD_DIM ** (-0.5)
    scores = scores.reshape(rows, query_local, count)
    allowed_wide = allowed[:, None, :]
    masked = jnp.where(allowed_wide, scores, NEG_BIG)
    new_best = jnp.maximum(best, jnp.max(masked, axis=2))
    weights = jnp.where(allowed_wide, jnp.exp(masked - new_best[:, :, None]), 0.0)
    total = jnp.sum(weights, axis=2)
    update = jnp.einsum(
        "tkgr,rkd->tkgd",
        weights.astype(jnp.bfloat16).reshape(rows, kv_local, group_size, count),
        value_piece.reshape(count, kv_local, HEAD_DIM),
        preferred_element_type=jnp.float32,
    )
    accum = update.reshape(rows, query_local, HEAD_DIM)
    folded = (new_best, total, accum)
    total = folded[1]
    accum = folded[2]
    safe_total = jnp.where(live_rows[:, None], total, 1.0)
    head_out = (
        (accum / safe_total[:, :, None] * live[:, None, None])
        .astype(jnp.bfloat16)
        .reshape(rows, query_local * HEAD_DIM)
    )
    return (layer_out, head_out)


def solution(mesh):
    placed = (
        P("doc"),
        P(("doc", "seq"), "head"),
        P(("doc", "seq"), "head"),
        P(("doc", "seq"), None),
        P(("doc", "seq"), None),
        P(("doc", "head"), "seq"),
        P("head"),
        P("head"),
        P("head", None),
        P(),
        P(None, "head"),
        P(None, "head"),
        P(None, "head"),
    )
    return jax.shard_map(
        body,
        mesh=mesh,
        in_specs=placed,
        out_specs=(P(("doc", "seq"), "head"), P(("doc", "seq"), "head")),
        check_vma=False,
    )
```

profile of v0, /device:TPU:0, one launch (start us, length us, event | category | flops | bytes accessed | tf_op | source)
XLA Modules:
  0.0 233.8 jit_solution(13353778681474807331)
XLA Ops:
  8.7 0.8 multiply_bitcast_fusion.1
  10.5 1.2 copy.34
  11.9 2.3 fusion.31
  14.2 0.8 mul.159
  15.0 1.2 dynamic-slice
  17.1 8.4 %all-reduce = f32[64]{0:T(128)S(1)} all-reduce(f32[64]{0:T(128)S(1)} %dynamic-update-slice), channel_id=2, replica_groups=mesh['doc'=2,'seq'=4,'head'=4] {'seq'}, use_global_device_ids=true, to_apply=%add | all-reduce | flops 64 | bytes 512
  25.6 1.1 fusion.48
  26.7 4.4 %fusion.20 = f32[256,16,64]{0,2,1:T(8,128)} fusion(bf16[256,16,64]{0,2,1:T(8,128)(2,1)S(1)} %bitcast.100, f32[16,256]{1,0:T(8,128)S(1)} %get-tuple-element.130, f32[256,256]{1,0:T(8,128)S(1)} %fusion.48, f32[16,256]{1,0:T(8,128)S(1)} %copy_bitcast_fusion, pred[256,256]{1,0:T(8,128)(4,1)S(1)} %iota_compare_fusion.1), kind=kOutput, calls=%fused_computation.24 | convolution fusion | flops 810549248 | bytes 1933312 | tf_op jit(solution)/shard_map/hts,shp->thp/dot_general | solution.py:66
  31.1 8.5 %all-gather.7.cloned.1.call-done = f32[64,64,128]{2,1,0:T(8,128)} async-done(((f32[16,64,128]{2,1,0:T(8,128)}), f32[64,64,128]{2,1,0:T(8,128)}) %all-gather.7.cloned.1.call-update) | async-done | bytes 2097168 | tf_op jit(solution)/shard_map/all_gather | solution.py:16
  39.6 3.6 %while.14 = (s32[]{:T(128)}, f32[16,64,128]{2,1,0:T(8,128)S(1)}, s32[]{:T(128)}, f32[4,16]{1,0:T(4,128)S(1)}, f32[4,16,64,128]{3,2,1,0:T(8,128)}, /*index=5*/s32[]{:T(128)}, s32[]{:T(128)}) while((s32[]{:T(128)}, f32[16,64,128]{2,1,0:T(8,128)S(1)}, s32[]{:T(128)}, f32[4,16]{1,0:T(4,128)S(1)}, f32[4,16,64,128]{3,2,1,0:T(8,128)}, ...), condition=%wide.region_3.4_spmd.clone, body=%wide.region_2.3_spmd.clone.sunk | while | flops 524292 | bytes 1573169 | solution.py:25
  39.6 1.2 fusion.64
  40.8 1.2 fusion.64
  42.1 1.2 fusion.64
  43.2 1.9 multiply_reduce_fusion
  45.4 7.7 %fusion.49 = f32[256,4096]{1,0:T(8,128)} fusion(bf16[256,1024]{0,1:T(8,128)(2,1)S(1)} %bitcast.98, bf16[1024,4096]{1,0:T(8,128)(2,1)} %param.23), kind=kOutput, calls=%fused_computation.78 | convolution fusion | flops 2147483648 | bytes 13107200 | tf_op jit(solution)/shard_map/dot_general | solution.py:86
  53.9 76.2 %reduce-scatter.2.cloned.1.call-done = f32[256,1024]{1,0:T(8,128)} async-done(((f32[256,4096]{1,0:T(8,128)}), f32[256,1024]{1,0:T(8,128)}) %reduce-scatter.2.cloned.1.call-update) | async-done | bytes 1048592 | tf_op jit(solution)/shard_map/reduce_scatter | solution.py:89
  130.0 1.5 fusion.26
  131.5 11.0 %psum.7 = f32[256]{0:T(256)S(1)} all-reduce(f32[256]{0:T(256)S(1)} %get-tuple-element.127), channel_id=1, replica_groups=mesh['doc'=2,'seq'=4,'head'=4] {'head'}, use_global_device_ids=true, to_apply=%region_7.8 | all-reduce | flops 256 | bytes 2048 | tf_op jit(solution)/shard_map/psum | solution.py:92
  142.5 1.0 fusion.28
  143.8 43.9 %all-gather.5.cloned.1.call-done = bf16[256,4096]{1,0:T(8,128)(2,1)} async-done(((bf16[256,1024]{1,0:T(8,128)(2,1)}), bf16[256,4096]{1,0:T(8,128)(2,1)}) %all-gather.5.cloned.1.call-update) | async-done | bytes 2097168 | tf_op jit(solution)/shard_map/all_gather | solution.py:97
  187.7 6.3 %convolution_convert_fusion = bf16[256,1024]{1,0:T(8,128)(2,1)S(1)} fusion(bf16[256,4096]{1,0:T(8,128)(2,1)} %all-gather.5.cloned.1.call-done, bf16[4096,1024]{1,0:T(8,128)(2,1)} %param.25), kind=kOutput, calls=%fused_computation.30 | convolution fusion | flops 2147745792 | bytes 11010048 | tf_op jit(solution)/shard_map/dot_general | solution.py:98
  194.0 1.2 reshape.194
  195.2 2.3 convolution_convert_fusion.2
  197.5 7.2 %all_gather.23 = bf16[1024,256]{1,0:T(8,128)(2,1)S(1)} all-gather(bf16[256,256]{1,0:T(8,128)(2,1)S(1)} %convolution_convert_fusion.2), channel_id=1, replica_groups=mesh['doc'=2,'seq'=4,'head'=4] {'seq'}, dimensions={0}, use_global_device_ids=true | all-gather | bytes 655360 | tf_op jit(solution)/shard_map/all_gather | solution.py:109
  204.9 2.9 %convolution_convert_fusion.1 = bf16[256,256]{1,0:T(8,128)(2,1)S(1)} fusion(bf16[256,4096]{1,0:T(8,128)(2,1)} %all-gather.5.cloned.1.call-done, bf16[4096,256]{1,0:T(8,128)(2,1)} %param.26), kind=kOutput, calls=%fused_computation.31 | convolution fusion | flops 536936448 | bytes 4325376 | tf_op jit(solution)/shard_map/dot_general | solution.py:101
  207.8 7.5 %all_gather.24 = bf16[1024,256]{1,0:T(8,128)(2,1)S(1)} all-gather(bf16[256,256]{1,0:T(8,128)(2,1)S(1)} %convolution_convert_fusion.1), channel_id=1, replica_groups=mesh['doc'=2,'seq'=4,'head'=4] {'seq'}, dimensions={0}, use_global_device_ids=true | all-gather | bytes 655360 | tf_op jit(solution)/shard_map/all_gather | solution.py:108
  215.3 0.9 reshape.193
  216.2 2.7 %fusion.1 = (f32[256,2,4]{0,2,1:T(4,128)S(1)}, f32[2,1024,256,4]{2,1,3,0:T(8,128)S(1)}) fusion(pred[256,1024]{0,1:T(8,128)(4,1)S(1)} %fusion.34, bf16[256,2,4,128]{3,2,1,0:T(4,128)(2,1)} %reshape.194, bf16[1024,2,128,1]{2,1,0,3:T(2,128)(2,1)} %bitcast.103), kind=kOutput, calls=%fused_computation.5 | convolution fusion | flops 543160320 | bytes 9707520 | tf_op jit(solution)/shard_map/tkgd,rkd->tkgr/dot_general | solution.py:113
  218.9 2.0 fusion.2
  220.9 3.2 %fusion.11 = f32[2,128,256,4]{2,1,3,0:T(8,128)} fusion(bf16[1024,2,128,1]{0,2,3,1:T(8,128)(2,1)S(1)} %bitcast.102, f32[2,1024,256,4]{2,1,3,0:T(8,128)S(1)} %get-tuple-element.138, f32[256,2,4]{0,2,1:T(4,128)S(1)} %broadcast_maximum_fusion, pred[256,1024]{0,1:T(8,128)(4,1)S(1)} %fusion.34), kind=kOutput, calls=%fused_computation.15 | convolution fusion | flops 547356672 | bytes 10231808 | tf_op jit(solution)/shard_map/tkgr,rkd->tkgd/dot_general | solution.py:125
  224.1 1.6 copy.40
  226.2 1.0 fusion.30
  (45 shorter events, 4.2 us)
Async XLA Ops:
  7.2 188.0 %copy-start = (bf16[4096,256]{1,0:T(8,128)(2,1)S(1)}, bf16[4096,256]{1,0:T(8,128)(2,1)}, u32[]{:S(2)}) copy-start(bf16[4096,256]{1,0:T(8,128)(2,1)} %param.27) | copy-start | bytes 6291460
  7.2 32.4 %all-gather.7.cloned.1.call-start = ((), (), s32[]{:S(2)}) async-start(), calls=%async_computation.3 | async-start | bytes 2621440 | tf_op jit(solution)/shard_map/all_gather | solution.py:16
  14.2 115.8 %reduce-scatter.2.cloned.1.call-start = ((), (), s32[]{:S(2)}) async-start(), calls=%async_computation.1 | async-start | bytes 5242880 | tf_op jit(solution)/shard_map/reduce_scatter | solution.py:89
  31.1 12.2 %copy-start.3 = (bf16[256,128]{1,0:T(8,128)(2,1)S(1)}, bf16[256,128]{1,0:T(8,128)(2,1)}, u32[]{:S(2)}) copy-start(bf16[256,128]{1,0:T(8,128)(2,1)} %param.19) | copy-start | bytes 196612
  53.0 77.0 %copy-start.2 = (bf16[256,1024]{1,0:T(8,128)(2,1)S(1)}, bf16[256,1024]{1,0:T(8,128)(2,1)}, u32[]{:S(2)}) copy-start(bf16[256,1024]{1,0:T(8,128)(2,1)} %param.16) | copy-start | bytes 1572868
  53.1 134.6 %all-gather.5.cloned.1.call-start = ((), (), s32[]{:S(2)}) async-start(), calls=%async_computation.2 | async-start | bytes 2621440 | tf_op jit(solution)/shard_map/all_gather | solution.py:97
  131.5 62.5 %copy-start.1 = (bf16[256,1024]{1,0:T(8,128)(2,1)}, bf16[256,1024]{1,0:T(8,128)(2,1)S(1)}, u32[]{:S(2)}) copy-start(bf16[256,1024]{1,0:T(8,128)(2,1)S(1)} %get-tuple-element.128) | copy-start | bytes 1572868
Sparse Core Ops, SparseCore 0:
  14.3 25.2 all-gather.6
  53.2 76.7 reduce-scatter.1
  143.6 43.9 all-gather.4
where the time goes:
time: 235 us; the launch traced here: 234 us
  waiting for transfers between devices  129 us (55%)
  matrix products  34.8 us (15%)
  blocking collectives  34 us (14%)
  between operations  15.4 us (7%)
  other arithmetic  11.7 us (5%)
  local copies, waits for them, and re-layouts  9.02 us (4%)
    reduce_scatter x1, waiting for transfers between devices, body(): lax.psum_scatter(partial_value, 'head', scatter_dimension=1, tiled=True)  76.2 us
    all_gather x1, waiting for transfers between devices, body(): attn_in = lax.all_gather(scaled, 'head', axis=1, tiled=True)  43.9 us
    psum x1, blocking collectives, body(): squares = lax.psum(jnp.sum(widened * widened, axis=1), 'head')  11 us
    all_gather x1, waiting for transfers between devices, prefix_2(): pieces = jax.tree.map(lambda part: lax.all_gather(part, axis), value)  8.54 us
    unnamed x1, blocking collectives  8.37 us
    dot_general x1, matrix products, body(): jnp.dot(normed, out_weight, preferred_element_type=jnp.float32)  7.69 us
    all_gather x1, blocking collectives, body(): key_piece = lax.all_gather(keys, 'seq', axis=0, tiled=True)  7.46 us
    all_gather x1, blocking collectives, body(): value_piece = lax.all_gather(values, 'seq', axis=0, tiled=True)  7.15 us
  transfers between devices with their start and end apart: 3, of which 3 were waited for; matrix products, arithmetic and copies ran while one was open for 4% of the time, Pallas kernels for 0%

commit v1 on v0

--- a/solution.py
+++ b/solution.py
@@ -11,22 +11,59 @@
 HIGHEST = lax.Precision.HIGHEST
 
 
-def prefix_2(value, axis, join, neutral):
-    count, mine = (lax.axis_size(axis), lax.axis_index(axis))
-    pieces = jax.tree.map(lambda part: lax.all_gather(part, axis), value)
-    so_far = jax.tree.map(
-        lambda part, zero: jnp.full_like(part, 0) + jnp.asarray(zero, part.dtype), value, neutral
-    )
-
-    def turn(position, so_far):
-        longer = join(so_far, jax.tree.map(lambda part: part[position], pieces))
-        return jax.tree.map(lambda new, old: jnp.where(position < mine, new, old), longer, so_far)
-
-    return lax.fori_loop(0, count - 1, turn, so_far)
+def split_3(value):
+    high = lax.reduce_precision(value, 8, 7)
+    middle = lax.reduce_precision(value - high, 8, 7)
+    low = value - high - middle
+    return jnp.stack([high, middle, low], axis=1).astype(jnp.bfloat16)
 
 
-def chain_link(earlier, later):
-    return (earlier[0] * later[0], later[0][:, None, None] * earlier[1] + later[1])
+def incoming_state(log_decay, local_state, axis):
+    count, mine = (lax.axis_size(axis), lax.axis_index(axis))
+    heads, width, states = local_state.shape
+    decay_rows = jnp.pad(split_3(log_decay), ((0, 0), (0, states - 3)))
+    packed = jnp.concatenate(
+        [local_state.astype(jnp.bfloat16).reshape(heads * width, states), decay_rows], axis=0
+    )
+    pieces = lax.all_gather(packed, axis)
+    logs = jnp.sum(pieces[:, heads * width :, :3].astype(jnp.float32), axis=2)
+    order = jnp.arange(count)
+    between = (order[None, :] > order[:, None]) & (order[None, :] < mine)
+    reach = jnp.sum(jnp.where(between[:, :, None], logs[None], 0.0), axis=1)
+    factor = jnp.where((order < mine)[:, None], jnp.exp(reach), 0.0)
+    total = jnp.zeros(local_state.shape, jnp.float32)
+    for position in range(count - 1):
+        piece = pieces[position, : heads * width].reshape(heads, width, states)
+        total += factor[position][:, None, None] * piece.astype(jnp.float32)
+    return total
+
+
+def chain_scatter(partial_value, axis):
+    count, mine = (lax.axis_size(axis), lax.axis_index(axis))
+    width = partial_value.shape[1] // count
+
+    def block(index):
+        start = jnp.clip(index, 0, count - 1) * width
+        return lax.dynamic_slice_in_dim(partial_value, start, width, axis=1)
+
+    up = down = None
+    for step in range(count - 1):
+        own_up = block(count - 1 - step + mine)
+        own_down = block(step - (count - 1 - mine))
+        send_up = own_up if up is None else own_up + up.astype(jnp.float32)
+        send_down = own_down if down is None else own_down + down.astype(jnp.float32)
+        up = lax.ppermute(
+            send_up.astype(jnp.bfloat16), axis, [(z, z + 1) for z in range(step + 1)]
+        )
+        down = lax.ppermute(
+            send_down.astype(jnp.bfloat16),
+            axis,
+            [(count - 1 - z, count - 2 - z) for z in range(step + 1)],
+        )
+    total = block(mine)
+    if up is not None:
+        total = total + up.astype(jnp.float32) + down.astype(jnp.float32)
+    return total
 
 
 def body(
@@ -68,14 +105,7 @@
     local_state = jnp.einsum(
         "hs,shp,sn->hpn", tail, inputs, state_in.astype(jnp.float32), precision=HIGHEST
     )
-    block_decay = jnp.exp(cumlog[:, -1])
-    prefix = prefix_2(
-        (block_decay, local_state),
-        "seq",
-        chain_link,
-        (jnp.ones_like(block_decay), jnp.zeros_like(local_state)),
-    )
-    incoming = prefix[1]
+    incoming = incoming_state(cumlog[:, -1], local_state, "seq")
     carried = jnp.einsum("hpn,tn->thp", incoming, state_out.astype(jnp.float32), precision=HIGHEST)
     ssm_out = (within + jnp.exp(cumlog).T[:, :, None] * carried) * live[:, None, None]
     mean_square = jnp.mean(ssm_out * ssm_out, axis=2, keepdims=True)
@@ -84,17 +114,11 @@
     ).astype(jnp.bfloat16)
     normed = normed.reshape(rows, local_heads * head_width)
     partial_value = jnp.dot(normed, out_weight, preferred_element_type=jnp.float32)
-    model_width = norm_gain.shape[0]
-    own_width = residual.shape[1]
-    projected = lax.psum_scatter(partial_value, "head", scatter_dimension=1, tiled=True)
+    projected = chain_scatter(partial_value, "head")
     layer_out = (residual.astype(jnp.float32) + projected).astype(jnp.bfloat16)
-    widened = layer_out.astype(jnp.float32)
-    squares = lax.psum(jnp.sum(widened * widened, axis=1), "head")
-    piece_gain = lax.dynamic_slice_in_dim(norm_gain, lax.axis_index("head") * own_width, own_width)
-    scaled = (widened * lax.rsqrt(squares / model_width + EPSILON)[:, None] * piece_gain).astype(
-        jnp.bfloat16
-    )
-    attn_in = lax.all_gather(scaled, "head", axis=1, tiled=True)
+    widened = lax.all_gather(layer_out, "head", axis=1, tiled=True).astype(jnp.float32)
+    squares = jnp.mean(widened * widened, axis=1, keepdims=True)
+    attn_in = (widened * lax.rsqrt(squares + EPSILON) * norm_gain).astype(jnp.bfloat16)
     queries = jnp.dot(attn_in, query_weight, preferred_element_type=jnp.float32).astype(
         jnp.bfloat16
     )
@@ -105,8 +129,11 @@
     group_size = query_local // kv_local
     grouped = queries.reshape(rows, kv_local, group_size, HEAD_DIM)
     best = jnp.full((rows, query_local), NEG_BIG, jnp.float32)
-    key_piece = lax.all_gather(keys, "seq", axis=0, tiled=True)
-    value_piece = lax.all_gather(values, "seq", axis=0, tiled=True)
+    key_value = lax.all_gather(
+        jnp.concatenate([keys, values], axis=1), "seq", axis=0, tiled=True
+    )
+    key_piece = key_value[:, : keys.shape[1]]
+    value_piece = key_value[:, keys.shape[1] :]
     count = key_piece.shape[0]
     key_pos = jnp.arange(count, dtype=jnp.int32)
     allowed = (key_pos[None, :] <= positions[:, None]) & (key_pos[None, :] < limit)

time: 235 us -> 201 us (0.86)
  blocking collectives: 34 us -> 0 us
  waiting for transfers between devices: 129 us -> 107 us
  starting transfers between devices: 0.12 us -> 18.5 us
  other arithmetic: 11.7 us -> 19.1 us
  matrix products: 34.8 us -> 30 us
    reduce_scatter x1 -> x0, waiting for transfers between devices: 76.2 us -> none  [body(): lax.psum_scatter(partial_value, 'head', scatter_dimension=1, tiled=True)]
    ppermute x0 -> x6, waiting for transfers between devices: none -> 40.9 us  [the longest x3 26.1 us: chain_scatter(): lax.ppermute(send_up.astype(jnp.bfloat16), axis, [(z, z + 1) for z in ran...]
    ppermute x0 -> x6, starting transfers between devices: none -> 18.2 us  [the longest x3 14.6 us: chain_scatter(): lax.ppermute(send_up.astype(jnp.bfloat16), axis, [(z, z + 1) for z in ran...]
    all_gather x2 -> x0, blocking collectives: 14.6 us -> none  [the longest x1 7.46 us: body(): key_piece = lax.all_gather(keys, 'seq', axis=0, tiled=True)]
    all_gather x2 -> x3, waiting for transfers between devices: 52.4 us -> 66.4 us  [the longest x1 44.3 us: body(): lax.all_gather(layer_out, 'head', axis=1, tiled=True).astype(jnp.float32)]
    psum x1 -> x0, blocking collectives: 11 us -> none  [body(): squares = lax.psum(jnp.sum(widened * widened, axis=1), 'head')]
    unnamed x1 -> x0, blocking collectives: 8.37 us -> none
    convert_element_type x1 -> x4, other arithmetic: 0.99 us -> 8.69 us  [the longest x2 4.37 us: chain_scatter(): send_up.astype(jnp.bfloat16)]
  transfers between devices with their start and end apart: 3 -> 9, of which waited for: 3 -> 7; matrix products, arithmetic and copies ran while one was open for 4% -> 8% of each run, Pallas kernels for 0% -> 0%
where the time goes in v1:
time: 201 us; the launch traced here: 200 us
  waiting for transfers between devices  107 us (53%)
  matrix products  30 us (15%)
  other arithmetic  19.1 us (10%)
  starting transfers between devices  18.5 us (9%)
  between operations  14.8 us (7%)
  local copies, waits for them, and re-layouts  10.2 us (5%)
    all_gather x1, waiting for transfers between devices, body(): lax.all_gather(layer_out, 'head', axis=1, tiled=True).astype(jnp.float32)  44.3 us
    ppermute x3, waiting for transfers between devices, chain_scatter(): lax.ppermute(send_up.astype(jnp.bfloat16), axis, [(z, z + 1) for z in ran...  26.1 us
    ppermute x3, waiting for transfers between devices, chain_scatter(): lax.ppermute(send_down.astype(jnp.bfloat16), axis, [(count - 1 - z, count...  14.8 us
    ppermute x3, starting transfers between devices, chain_scatter(): lax.ppermute(send_up.astype(jnp.bfloat16), axis, [(z, z + 1) for z in ran...  14.6 us
    all_gather x1, waiting for transfers between devices, incoming_state(): pieces = lax.all_gather(packed, axis)  13.3 us
    all_gather x1, waiting for transfers between devices, body(): lax.all_gather(jnp.concatenate([keys, values], axis=1), 'seq', axis=0, ti...  8.75 us
    dot_general x1, matrix products, body(): jnp.dot(attn_in, query_weight, preferred_element_type=jnp.float32)  6.4 us
    dot_general x1, matrix products, body(): jnp.dot(normed, out_weight, preferred_element_type=jnp.float32)  5.92 us
  transfers between devices with their start and end apart: 9, of which 7 were waited for; matrix products, arithmetic and copies ran while one was open for 8% of the time, Pallas kernels for 0%

profile of v1, /device:TPU:0, one launch (start us, length us, event | category | flops | bytes accessed | tf_op | source)
XLA Modules:
  0.0 199.9 jit_solution(4303016293539564433)
XLA Ops:
  10.6 1.2 copy.56
  12.0 1.5 convolution_convert_fusion.1
  16.2 4.4 %fusion.22 = f32[256,16,64]{0,2,1:T(8,128)} fusion(bf16[256,16,64]{0,2,1:T(8,128)(2,1)S(1)} %bitcast.103, f32[16,256]{1,0:T(8,128)S(1)} %get-tuple-element.3, f32[256,256]{1,0:T(8,128)S(1)} %fusion.61, f32[16,256]{1,0:T(8,128)S(1)} %copy_bitcast_fusion, pred[256,256]{1,0:T(8,128)(4,1)S(1)} %iota_compare_fusion.2), kind=kOutput, calls=%fused_computation.26 | convolution fusion | flops 810549248 | bytes 1933312 | tf_op jit(solution)/shard_map/hts,shp->thp/dot_general | solution.py:103
  20.6 13.3 %all-gather.9.cloned.1.call-done = bf16[4160,128]{1,0:T(8,128)(2,1)} async-done(((bf16[1040,128]{1,0:T(8,128)(2,1)}), bf16[4160,128]{1,0:T(8,128)(2,1)}) %all-gather.9.cloned.1.call-update) | async-done | bytes 1064976 | tf_op jit(solution)/shard_map/all_gather | solution.py:28
  34.7 1.2 fusion.59
  36.0 2.0 multiply_reduce_fusion
  38.2 5.9 %fusion.62 = f32[256,4096]{1,0:T(8,128)S(1)} fusion(bf16[256,1024]{0,1:T(8,128)(2,1)S(1)} %bitcast.101, bf16[1024,4096]{1,0:T(8,128)(2,1)} %param.21), kind=kOutput, calls=%fused_computation.107 | convolution fusion | flops 2147483648 | bytes 13107200 | tf_op jit(solution)/shard_map/dot_general | solution.py:116
  44.2 1.9 copy-done.1
  47.0 4.2 %collective-permute-start = (bf16[256,1024]{1,0:T(8,128)(2,1)S(1)}, bf16[256,1024]{1,0:T(8,128)(2,1)}, u32[]{:S(2)}, u32[]{:S(2)}) collective-permute-start(bf16[256,1024]{1,0:T(8,128)(2,1)S(1)} %get-tuple-element.8), channel_id=1, source_target_pairs={{0,1},{4,5},{8,9},{12,13},{16,17},{20,21},{24,25},{28,29}} | collective-permute-start | bytes 1572872 | tf_op jit(solution)/shard_map/ppermute | solution.py:55
  51.9 10.1 %collective-permute-done = bf16[256,1024]{1,0:T(8,128)(2,1)} collective-permute-done((bf16[256,1024]{1,0:T(8,128)(2,1)S(1)}, bf16[256,1024]{1,0:T(8,128)(2,1)}, u32[]{:S(2)}, u32[]{:S(2)}) %collective-permute-start) | collective-permute-done | bytes 524320 | tf_op jit(solution)/shard_map/ppermute | solution.py:55
  62.0 1.5 add_convert_fusion.4
  63.5 5.3 %collective-permute-start.1 = (bf16[256,1024]{1,0:T(8,128)(2,1)S(1)}, bf16[256,1024]{1,0:T(8,128)(2,1)}, u32[]{:S(2)}, u32[]{:S(2)}) collective-permute-start(bf16[256,1024]{1,0:T(8,128)(2,1)S(1)} %add_convert_fusion.4), channel_id=1, source_target_pairs={{0,1},{1,2},{4,5},{5,6},{8,9},{9,10},{12,13},{13,14},{16,17},{17,1... | collective-permute-start | bytes 1572872 | tf_op jit(solution)/shard_map/ppermute | solution.py:55
  68.8 9.9 %collective-permute-done.1 = bf16[256,1024]{1,0:T(8,128)(2,1)} collective-permute-done((bf16[256,1024]{1,0:T(8,128)(2,1)S(1)}, bf16[256,1024]{1,0:T(8,128)(2,1)}, u32[]{:S(2)}, u32[]{:S(2)}) %collective-permute-start.1) | collective-permute-done | bytes 524320 | tf_op jit(solution)/shard_map/ppermute | solution.py:55
  78.7 2.8 %add_convert_fusion.3 = (bf16[256,1024]{1,0:T(8,128)(2,1)S(1)}, bf16[256,1024]{1,0:T(8,128)(2,1)}) fusion(bf16[256,1024]{1,0:T(8,128)(2,1)} %collective-permute-done.1, f32[256,4096]{1,0:T(8,128)} %copy-done.1, s32[]{:T(128)S(6)} %select_n.66, bf16[256,1024]{1,0:T(8,128)(2,1)S(1)} %collective-permute-done.3, s32[]{:T(128)S(6)} %select_n.70), kind=kLoop, calls=%fused_computation.42 | loop fusion | flops 1572864 | bytes 4194312 | tf_op jit(solution)/shard_map/convert_element_type | solution.py:56
  81.6 1.6 collective-permute-start.4
  83.2 5.1 %collective-permute-start.2 = (bf16[256,1024]{1,0:T(8,128)(2,1)S(1)}, bf16[256,1024]{1,0:T(8,128)(2,1)}, u32[]{:S(2)}, u32[]{:S(2)}) collective-permute-start(bf16[256,1024]{1,0:T(8,128)(2,1)S(1)} %get-tuple-element.6), channel_id=1, source_target_pairs={{0,1},{1,2},{2,3},{4,5},{5,6},{6,7},{8,9},{9,10},{10,11},{12,13},{... | collective-permute-start | bytes 1572872 | tf_op jit(solution)/shard_map/ppermute | solution.py:55
  88.3 1.5 add_convert_fusion.1
  89.8 1.3 collective-permute-start.5
  91.1 6.2 %collective-permute-done.2 = bf16[256,1024]{1,0:T(8,128)(2,1)} collective-permute-done((bf16[256,1024]{1,0:T(8,128)(2,1)S(1)}, bf16[256,1024]{1,0:T(8,128)(2,1)}, u32[]{:S(2)}, u32[]{:S(2)}) %collective-permute-start.2) | collective-permute-done | bytes 524320 | tf_op jit(solution)/shard_map/ppermute | solution.py:55
  97.3 14.8 %collective-permute-done.5 = bf16[256,1024]{1,0:T(8,128)(2,1)} collective-permute-done((bf16[256,1024]{1,0:T(8,128)(2,1)S(1)}, bf16[256,1024]{1,0:T(8,128)(2,1)}, u32[]{:S(2)}, u32[]{:S(2)}) %collective-permute-start.5) | collective-permute-done | bytes 524320 | tf_op jit(solution)/shard_map/ppermute | solution.py:58
  112.1 2.8 %add_convert_fusion = bf16[256,1024]{1,0:T(8,128)(2,1)} fusion(bf16[256,1024]{1,0:T(8,128)(2,1)} %collective-permute-done.5, bf16[256,1024]{1,0:T(8,128)(2,1)} %collective-permute-done.2, f32[256,4096]{1,0:T(8,128)} %copy-done.1, s32[]{:T(128)S(6)} %select_n.65, bf16[256,1024]{1,0:T(8,128)(2,1)} %param.14), kind=kLoop, calls=%fused_computation.38 | loop fusion | flops 1835008 | bytes 3145732 | tf_op jit(solution)/shard_map/convert_element_type | solution.py:118
  115.1 44.3 %all-gather.5.cloned.1.call-done = bf16[256,4096]{1,0:T(8,128)(2,1)} async-done(((bf16[256,1024]{1,0:T(8,128)(2,1)}), bf16[256,4096]{1,0:T(8,128)(2,1)}) %all-gather.5.cloned.1.call-update) | async-done | bytes 2097168 | tf_op jit(solution)/shard_map/all_gather | solution.py:119
  159.4 2.2 %fusion.3 = f32[256]{0:T(256)S(1)} fusion(bf16[256,4096]{1,0:T(8,128)(2,1)} %all-gather.5.cloned.1.call-done), kind=kLoop, calls=%fused_computation.7 | loop fusion | flops 3145472 | bytes 2098176 | tf_op jit(solution)/shard_map/reduce_sum | solution.py:120
  161.7 2.7 %convolution_convert_fusion.2 = bf16[256,256]{0,1:T(8,128)(2,1)S(1)} fusion(bf16[4096,256]{1,0:T(8,128)(2,1)S(1)} %copy-done, bf16[256,4096]{1,0:T(8,128)(2,1)} %all-gather.5.cloned.1.call-done, f32[4096]{0:T(1024)S(1)} %copy-done.5, f32[256]{0:T(256)S(1)} %add_rsqrt_fusion.1), kind=kOutput, calls=%fused_computation.32 | convolution fusion | flops 541130752 | bytes 4342784 | tf_op jit(solution)/shard_map/dot_general | solution.py:126
  164.5 1.2 convolution_convert_fusion.3
  166.7 6.4 %convolution_convert_fusion = bf16[256,1024]{1,0:T(8,128)(2,1)S(1)} fusion(bf16[4096,1024]{1,0:T(8,128)(2,1)} %param.23, bf16[256,4096]{1,0:T(8,128)(2,1)} %all-gather.5.cloned.1.call-done, f32[4096]{0:T(1024)S(1)} %copy-done.5, f32[256]{0:T(256)S(1)} %add_rsqrt_fusion.1), kind=kOutput, calls=%fused_computation.30 | convolution fusion | flops 2151940096 | bytes 11027456 | tf_op jit(solution)/shard_map/dot_general | solution.py:122
  173.4 8.8 %all-gather.7.cloned.1.call-done = bf16[1024,512]{0,1:T(8,128)(2,1)} async-done(((bf16[256,512]{0,1:T(8,128)(2,1)}), bf16[1024,512]{0,1:T(8,128)(2,1)}) %all-gather.7.cloned.1.call-update) | async-done | bytes 1048592 | tf_op jit(solution)/shard_map/all_gather | solution.py:132
  182.2 1.3 fusion.60
  183.5 1.6 fusion
  185.1 2.0 %fusion.1 = f32[256,2,4]{0,2,1:T(4,128)S(1)} fusion(f32[2,1024,256,4]{2,1,3,0:T(8,128)S(1)} %get-tuple-element.26, f32[256,2,4]{0,2,1:T(4,128)S(1)} %broadcast_maximum_fusion, pred[256,1024]{0,1:T(8,128)(4,1)S(1)} %fusion.32), kind=kLoop, calls=%fused_computation.3 | loop fusion | flops 10483712 | bytes 8667136 | tf_op jit(solution)/shard_map/reduce_sum | solution.py:151
  187.1 3.2 %fusion.13 = f32[2,128,256,4]{2,1,3,0:T(8,128)} fusion(bf16[1024,2,128,1]{0,2,3,1:T(8,128)(2,1)S(1)} %bitcast.112, f32[2,1024,256,4]{2,1,3,0:T(8,128)S(1)} %get-tuple-element.26, f32[256,2,4]{0,2,1:T(4,128)S(1)} %broadcast_maximum_fusion, pred[256,1024]{0,1:T(8,128)(4,1)S(1)} %fusion.32), kind=kOutput, calls=%fused_computation.17 | convolution fusion | flops 547356672 | bytes 10231808 | tf_op jit(solution)/shard_map/tkgr,rkd->tkgd/dot_general | solution.py:152
  190.3 1.6 copy.63
  (60 shorter events, 11.3 us)
Async XLA Ops:
  7.2 154.5 %copy-start = (bf16[4096,256]{1,0:T(8,128)(2,1)S(1)}, bf16[4096,256]{1,0:T(8,128)(2,1)}, u32[]{:S(2)}) copy-start(bf16[4096,256]{1,0:T(8,128)(2,1)} %param.25) | copy-start | bytes 6291460
  7.2 26.7 %all-gather.9.cloned.1.call-start = ((), (), s32[]{:S(2)}) async-start(), calls=%async_computation.2 | async-start | bytes 1331200 | tf_op jit(solution)/shard_map/all_gather | solution.py:28
  14.2 145.2 %all-gather.5.cloned.1.call-start = ((), (), s32[]{:S(2)}) async-start(), calls=%async_computation | async-start | bytes 2621440 | tf_op jit(solution)/shard_map/all_gather | solution.py:119
  16.1 19.9 %copy-start.3 = (bf16[256,128]{1,0:T(8,128)(2,1)S(1)}, bf16[256,128]{1,0:T(8,128)(2,1)}, u32[]{:S(2)}) copy-start(bf16[256,128]{1,0:T(8,128)(2,1)} %param.17) | copy-start | bytes 196612
  44.2 1.9 copy-start.1
  47.0 14.9 %collective-permute-start = (bf16[256,1024]{1,0:T(8,128)(2,1)S(1)}, bf16[256,1024]{1,0:T(8,128)(2,1)}, u32[]{:S(2)}, u32[]{:S(2)}) collective-permute-start(bf16[256,1024]{1,0:T(8,128)(2,1)S(1)} %get-tuple-element.8), channel_id=1, source_target_pairs={{0,1},{4,5},{8,9},{12,13},{16,17},{20,21},{24,25},{28,29}} | collective-permute-start | bytes 1572872 | tf_op jit(solution)/shard_map/ppermute | solution.py:55
  51.2 17.6 %collective-permute-start.3 = (bf16[256,1024]{1,0:T(8,128)(2,1)}, bf16[256,1024]{1,0:T(8,128)(2,1)S(1)}, u32[]{:S(2)}, u32[]{:S(2)}) collective-permute-start(bf16[256,1024]{1,0:T(8,128)(2,1)} %get-tuple-element.9), channel_id=1, source_target_pairs={{3,2},{7,6},{11,10},{15,14},{19,18},{23,22},{27,26},{31,30}} | collective-permute-start | bytes 1572872 | tf_op jit(solution)/shard_map/ppermute | solution.py:58
  63.5 15.2 %collective-permute-start.1 = (bf16[256,1024]{1,0:T(8,128)(2,1)S(1)}, bf16[256,1024]{1,0:T(8,128)(2,1)}, u32[]{:S(2)}, u32[]{:S(2)}) collective-permute-start(bf16[256,1024]{1,0:T(8,128)(2,1)S(1)} %add_convert_fusion.4), channel_id=1, source_target_pairs={{0,1},{1,2},{4,5},{5,6},{8,9},{9,10},{12,13},{13,14},{16,17},{17,1... | collective-permute-start | bytes 1572872 | tf_op jit(solution)/shard_map/ppermute | solution.py:55
  81.6 80.1 %copy-start.5 = (f32[4096]{0:T(1024)S(1)}, f32[4096]{0:T(1024)}, u32[]{:S(2)}) copy-start(f32[4096]{0:T(1024)} %param.22) | copy-start | bytes 49156
  81.6 6.7 %collective-permute-start.4 = (bf16[256,1024]{1,0:T(8,128)(2,1)}, bf16[256,1024]{1,0:T(8,128)(2,1)}, u32[]{:S(2)}, u32[]{:S(2)}) collective-permute-start(bf16[256,1024]{1,0:T(8,128)(2,1)} %get-tuple-element.7), channel_id=1, source_target_pairs={{3,2},{2,1},{7,6},{6,5},{11,10},{10,9},{15,14},{14,13},{19,18},{18... | collective-permute-start | bytes 1572872 | tf_op jit(solution)/shard_map/ppermute | solution.py:58
  83.2 14.2 %collective-permute-start.2 = (bf16[256,1024]{1,0:T(8,128)(2,1)S(1)}, bf16[256,1024]{1,0:T(8,128)(2,1)}, u32[]{:S(2)}, u32[]{:S(2)}) collective-permute-start(bf16[256,1024]{1,0:T(8,128)(2,1)S(1)} %get-tuple-element.6), channel_id=1, source_target_pairs={{0,1},{1,2},{2,3},{4,5},{5,6},{6,7},{8,9},{9,10},{10,11},{12,13},{... | collective-permute-start | bytes 1572872 | tf_op jit(solution)/shard_map/ppermute | solution.py:55
  89.8 22.3 %collective-permute-start.5 = (bf16[256,1024]{1,0:T(8,128)(2,1)S(1)}, bf16[256,1024]{1,0:T(8,128)(2,1)}, u32[]{:S(2)}, u32[]{:S(2)}) collective-permute-start(bf16[256,1024]{1,0:T(8,128)(2,1)S(1)} %add_convert_fusion.1), channel_id=1, source_target_pairs={{3,2},{2,1},{1,0},{7,6},{6,5},{5,4},{11,10},{10,9},{9,8},{15,14},{... | collective-permute-start | bytes 1572872 | tf_op jit(solution)/shard_map/ppermute | solution.py:58
  114.9 67.3 %all-gather.7.cloned.1.call-start = ((), (), s32[]{:S(2)}) async-start(), calls=%async_computation.1 | async-start | bytes 1310720 | tf_op jit(solution)/shard_map/all_gather | solution.py:132
  159.4 5.0 %copy-start.2 = (bf16[256,4096]{1,0:T(8,128)(2,1)S(1)}, bf16[256,4096]{1,0:T(8,128)(2,1)}, u32[]{:S(2)}) copy-start(bf16[256,4096]{1,0:T(8,128)(2,1)} %all-gather.5.cloned.1.call-done) | copy-start | bytes 6291460
  159.4 5.0 %copy-start.4 = (bf16[4096,256]{1,0:T(8,128)(2,1)S(1)}, bf16[4096,256]{1,0:T(8,128)(2,1)}, u32[]{:S(2)}) copy-start(bf16[4096,256]{1,0:T(8,128)(2,1)} %param.24) | copy-start | bytes 6291460
Sparse Core Ops, SparseCore 0:
  14.3 19.5 all-gather.8
  115.0 44.3 all-gather.4
  166.5 15.6 all-gather.6

commit v2 on v1

--- a/solution.py
+++ b/solution.py
@@ -1,6 +1,10 @@
+import functools
+
 import jax
 import jax.numpy as jnp
 from jax import lax
+from jax.experimental import pallas as pl
+from jax.experimental.pallas import tpu as pltpu
 from jax.sharding import PartitionSpec as P
 
 HEAD_DIM = 128
@@ -38,32 +42,206 @@
     return total
 
 
-def chain_scatter(partial_value, axis):
-    count, mine = (lax.axis_size(axis), lax.axis_index(axis))
-    width = partial_value.shape[1] // count
-
-    def block(index):
-        start = jnp.clip(index, 0, count - 1) * width
-        return lax.dynamic_slice_in_dim(partial_value, start, width, axis=1)
-
-    up = down = None
-    for step in range(count - 1):
-        own_up = block(count - 1 - step + mine)
-        own_down = block(step - (count - 1 - mine))
-        send_up = own_up if up is None else own_up + up.astype(jnp.float32)
-        send_down = own_down if down is None else own_down + down.astype(jnp.float32)
-        up = lax.ppermute(
-            send_up.astype(jnp.bfloat16), axis, [(z, z + 1) for z in range(step + 1)]
+def line_kernel(
+    count,
+    chunks,
+    partial_ref,
+    residual_ref,
+    gain_ref,
+    layer_ref,
+    attn_ref,
+    stage_ref,
+    landed_ref,
+    gathered_ref,
+    total_ref,
+    sum_send,
+    sum_recv,
+    copy_send,
+    copy_recv,
+):
+    mine = lax.axis_index("head")
+    last = count - 1
+    width = residual_ref.shape[1]
+    rows = residual_ref.shape[0] // chunks
+    place = (mine, last - mine)
+
+    barrier = pltpu.get_barrier_semaphore()
+
+    def greet(neighbour):
+        pl.semaphore_signal(
+            barrier, inc=1, device_id={"head": neighbour}, device_id_type=pl.DeviceIdType.MESH
         )
-        down = lax.ppermute(
-            send_down.astype(jnp.bfloat16),
-            axis,
-            [(count - 1 - z, count - 2 - z) for z in range(step + 1)],
+
+    @pl.when(mine > 0)
+    def _():
+        greet(mine - 1)
+
+    @pl.when(mine < last)
+    def _():
+        greet(mine + 1)
+
+    @pl.when((mine == 0) | (mine == last))
+    def _():
+        pl.semaphore_wait(barrier, 1)
+
+    @pl.when((mine > 0) & (mine < last))
+    def _():
+        pl.semaphore_wait(barrier, 2)
+
+    def neighbour(way):
+        return mine + 1 if way == 0 else mine - 1
+
+    def real(way, position):
+        return position if way == 0 else last - position
+
+    def sum_copy(way, chunk, step):
+        return pltpu.make_async_remote_copy(
+            src_ref=stage_ref.at[way, chunk, step],
+            dst_ref=landed_ref.at[way, chunk, step],
+            send_sem=sum_send.at[way, chunk, step],
+            recv_sem=sum_recv.at[way, chunk, step],
+            device_id={"head": neighbour(way)},
+            device_id_type=pl.DeviceIdType.MESH,
         )
-    total = block(mine)
-    if up is not None:
-        total = total + up.astype(jnp.float32) + down.astype(jnp.float32)
-    return total
+
+    def block_copy(way, chunk, step, source):
+        block = gathered_ref.at[source, pl.ds(chunk * rows, rows)]
+        return pltpu.make_async_remote_copy(
+            src_ref=block,
+            dst_ref=block,
+            send_sem=copy_send.at[way, chunk, step],
+            recv_sem=copy_recv.at[way, chunk, step],
+            device_id={"head": neighbour(way)},
+            device_id_type=pl.DeviceIdType.MESH,
+        )
+
+    def own_part(chunk, owner):
+        columns = pl.ds(pl.multiple_of(owner * width, 128), width)
+        return partial_ref[pl.ds(chunk * rows, rows), columns]
+
+    def sum_step(chunk, step):
+        for way in range(2):
+            owner = real(way, last - step + place[way])
+
+            @pl.when(place[way] == 0)
+            def _():
+                stage_ref[way, chunk, step] = own_part(chunk, owner).astype(jnp.bfloat16)
+                sum_copy(way, chunk, step).start()
+
+            if step == 0:
+                continue
+
+            @pl.when((place[way] <= step) & (place[way] > 0))
+            def _():
+                sum_copy(way, chunk, step - 1).wait_recv()
+                arrived = landed_ref[way, chunk, step - 1].astype(jnp.float32)
+                stage_ref[way, chunk, step] = (own_part(chunk, owner) + arrived).astype(
+                    jnp.bfloat16
+                )
+                sum_copy(way, chunk, step).start()
+
+    def finish_sum(chunk):
+        here = pl.ds(chunk * rows, rows)
+        total_ref[...] = residual_ref[here].astype(jnp.float32) + own_part(chunk, mine)
+        for way in range(2):
+
+            @pl.when(place[way] > 0)
+            def _():
+                sum_copy(way, chunk, last - 1).wait_recv()
+                total_ref[...] += landed_ref[way, chunk, last - 1].astype(jnp.float32)
+
+        layer_low = total_ref[...].astype(jnp.bfloat16)
+        gathered_ref[mine, here] = layer_low
+        layer_ref[here] = layer_low
+        for way in range(2):
+
+            @pl.when(place[way] < last)
+            def _():
+                block_copy(way, chunk, 0, mine).start()
+
+    def forward(chunk, step):
+        for way in range(2):
+            source = real(way, place[way] - step)
+
+            @pl.when(place[way] >= step)
+            def _():
+                block_copy(way, chunk, step - 1, source).wait_recv()
+
+            @pl.when((place[way] >= step) & (place[way] < last))
+            def _():
+                block_copy(way, chunk, step, source).start()
+
+    def normalise(chunk):
+        for way in range(2):
+
+            @pl.when(place[way] == last)
+            def _():
+                block_copy(way, chunk, last - 1, real(way, 0)).wait_recv()
+
+        here = pl.ds(chunk * rows, rows)
+        squares = jnp.zeros((rows, 1), jnp.float32)
+        for source in range(count):
+            block = gathered_ref[source, here].astype(jnp.float32)
+            squares += jnp.sum(block * block, axis=1, keepdims=True)
+        scale = lax.rsqrt(squares / (count * width) + EPSILON)
+        for source in range(count):
+            columns = slice(source * width, (source + 1) * width)
+            block = gathered_ref[source, here].astype(jnp.float32)
+            attn_ref[here, columns] = (block * scale * gain_ref[:, columns]).astype(jnp.bfloat16)
+
+    for tick in range(chunks + 2 * last):
+        for chunk in range(chunks):
+            stage = tick - chunk
+            if 0 <= stage < last:
+                sum_step(chunk, stage)
+            elif stage == last:
+                finish_sum(chunk)
+            elif last < stage < 2 * last:
+                forward(chunk, stage - last)
+            elif stage == 2 * last:
+                normalise(chunk)
+
+    for chunk in range(chunks):
+        for step in range(last):
+            for way in range(2):
+
+                @pl.when(place[way] <= step)
+                def _():
+                    sum_copy(way, chunk, step).wait_send()
+
+                @pl.when((place[way] >= step) & (place[way] < last))
+                def _():
+                    block_copy(way, chunk, step, real(way, place[way] - step)).wait_send()
+
+
+def line_sum_and_gather(partial_value, residual, norm_gain, count):
+    rows, width = residual.shape
+    chunks = 4 if rows % 64 == 0 else 1
+    steps = count - 1
+    piece = rows // chunks
+    messages = (2, chunks, steps)
+    return pl.pallas_call(
+        functools.partial(line_kernel, count, chunks),
+        out_shape=(
+            jax.ShapeDtypeStruct((rows, width), jnp.bfloat16),
+            jax.ShapeDtypeStruct((rows, width * count), jnp.bfloat16),
+        ),
+        in_specs=[pl.BlockSpec(memory_space=pltpu.VMEM)] * 3,
+        out_specs=[pl.BlockSpec(memory_space=pltpu.VMEM)] * 2,
+        scratch_shapes=[
+            pltpu.VMEM(messages + (piece, width), jnp.bfloat16),
+            pltpu.VMEM(messages + (piece, width), jnp.bfloat16),
+            pltpu.VMEM((count, rows, width), jnp.bfloat16),
+            pltpu.VMEM((piece, width), jnp.float32),
+            pltpu.SemaphoreType.DMA(messages),
+            pltpu.SemaphoreType.DMA(messages),
+            pltpu.SemaphoreType.DMA(messages),
+            pltpu.SemaphoreType.DMA(messages),
+        ],
+        compiler_params=pltpu.CompilerParams(
+            collective_id=0, has_side_effects=True, vmem_limit_bytes=40 * 1024 * 1024
+        ),
+    )(partial_value, residual, norm_gain.reshape(1, width * count))
 
 
 def body(
@@ -114,11 +292,9 @@
     ).astype(jnp.bfloat16)
     normed = normed.reshape(rows, local_heads * head_width)
     partial_value = jnp.dot(normed, out_weight, preferred_element_type=jnp.float32)
-    projected = chain_scatter(partial_value, "head")
-    layer_out = (residual.astype(jnp.float32) + projected).astype(jnp.bfloat16)
-    widened = lax.all_gather(layer_out, "head", axis=1, tiled=True).astype(jnp.float32)
-    squares = jnp.mean(widened * widened, axis=1, keepdims=True)
-    attn_in = (widened * lax.rsqrt(squares + EPSILON) * norm_gain).astype(jnp.bfloat16)
+    layer_out, attn_in = line_sum_and_gather(
+        partial_value, residual, norm_gain, lax.axis_size("head")
+    )
     queries = jnp.dot(attn_in, query_weight, preferred_element_type=jnp.float32).astype(
         jnp.bfloat16
     )

time: 201 us -> 147 us (0.73)
  waiting for transfers between devices: 107 us -> 19.9 us
  Pallas kernels: 0 us -> 62.7 us
  starting transfers between devices: 18.5 us -> 0.08 us
  other arithmetic: 19.1 us -> 9.43 us
    pallas_call x0 -> x1, Pallas kernels: none -> 62.7 us  [line_sum_and_gather(): pl.pallas_call(functools.partial(line_kernel, count, chunks), out_shape=(...]
    all_gather x1 -> x0, waiting for transfers between devices: 44.3 us -> none  [body(): lax.all_gather(layer_out, 'head', axis=1, tiled=True).astype(jnp.float32)]
    ppermute x6 -> x0, waiting for transfers between devices: 40.9 us -> none  [the longest x3 26.1 us: chain_scatter(): lax.ppermute(send_up.astype(jnp.bfloat16), axis, [(z, z + 1) for z in ran...]
    ppermute x6 -> x0, starting transfers between devices: 18.2 us -> none  [the longest x3 14.6 us: chain_scatter(): lax.ppermute(send_up.astype(jnp.bfloat16), axis, [(z, z + 1) for z in ran...]
    convert_element_type x4 -> x0, other arithmetic: 8.69 us -> none  [the longest x2 4.37 us: chain_scatter(): send_up.astype(jnp.bfloat16)]
    reduce_sum x1 -> x0, other arithmetic: 2.23 us -> none  [body(): squares = jnp.mean(widened * widened, axis=1, keepdims=True)]
    all_gather x1, waiting for transfers between devices: 8.75 us -> 6.55 us  [body(): lax.all_gather(jnp.concatenate([keys, values], axis=1), 'seq', axis=0, ti...]
  transfers between devices with their start and end apart: 9 -> 2, of which waited for: 7 -> 2; matrix products, arithmetic and copies ran while one was open for 8% -> 10% of each run, Pallas kernels for 0% -> 0%
where the time goes in v2:
time: 147 us; the launch traced here: 146 us
  Pallas kernels  62.7 us (43%)
  matrix products  28.6 us (19%)
  waiting for transfers between devices  19.9 us (14%)
  between operations  15.1 us (10%)
  local copies, waits for them, and re-layouts  10.2 us (7%)
  other arithmetic  9.43 us (6%)
    pallas_call x1, Pallas kernels, line_sum_and_gather(): pl.pallas_call(functools.partial(line_kernel, count, chunks), out_shape=(...  62.7 us
    all_gather x1, waiting for transfers between devices, incoming_state(): pieces = lax.all_gather(packed, axis)  13.3 us
    dot_general x1, matrix products, body(): jnp.dot(attn_in, query_weight, preferred_element_type=jnp.float32)  7.14 us
    all_gather x1, waiting for transfers between devices, body(): lax.all_gather(jnp.concatenate([keys, values], axis=1), 'seq', axis=0, ti...  6.55 us
    dot_general x1, matrix products, body(): jnp.dot(normed, out_weight, preferred_element_type=jnp.float32)  5.82 us
    dot_general x1, matrix products, body(): within = jnp.einsum('hts,shp->thp', mixing, inputs, precision=HIGHEST)  4.41 us
    dot_general x1, matrix products, body(): jnp.einsum('tkgr,rkd->tkgd', weights.astype(jnp.bfloat16).reshape(rows, k...  3.23 us
  transfers between devices with their start and end apart: 2, of which 2 were waited for; matrix products, arithmetic and copies ran while one was open for 10% of the time, Pallas kernels for 0%

profile of v2, /device:TPU:0, one launch (start us, length us, event | category | flops | bytes accessed | tf_op | source)
XLA Modules:
  0.0 145.9 jit_solution(1555734785623250953)
XLA Ops:
  8.0 0.7 neg.8
  8.7 0.8 multiply_bitcast_fusion.1
  9.5 0.6 reduce-window.6
  10.0 0.2 slice_reduce_fusion
  10.6 1.2 copy.56
  12.0 1.5 %convolution_convert_fusion.1 = bf16[16,64,128]{2,1,0:T(8,128)(2,1)S(1)} fusion(bf16[256,16,64]{0,2,1:T(8,128)(2,1)S(1)} %bitcast.107, f32[256,16]{0,1:T(8,128)S(1)} %get-tuple-element.16, bf16[256,128]{1,0:T(8,128)(2,1)} %param.16), kind=kOutput, calls=%fused_computation.26 | convolution fusion | flops 403308544 | bytes 868352 | tf_op jit(solution)/shard_map/hs,shp,sn->hpn/dot_general | solution.py:283
  13.5 0.7 fusion.38
  14.3 0.8 mul.152
  15.1 1.1 fusion.55
  16.1 4.4 %fusion.19 = f32[256,16,64]{0,2,1:T(8,128)} fusion(bf16[256,16,64]{0,2,1:T(8,128)(2,1)S(1)} %bitcast.108, f32[16,256]{1,0:T(8,128)S(1)} %get-tuple-element.7, f32[256,256]{1,0:T(8,128)S(1)} %fusion.55, f32[16,256]{1,0:T(8,128)S(1)} %copy_bitcast_fusion, pred[256,256]{1,0:T(8,128)(4,1)S(1)} %iota_compare_fusion.2), kind=kOutput, calls=%fused_computation.21 | convolution fusion | flops 810549248 | bytes 1933312 | tf_op jit(solution)/shard_map/hts,shp->thp/dot_general | solution.py:281
  20.6 13.3 %all-gather.6.cloned.1.call-done = bf16[4160,128]{1,0:T(8,128)(2,1)} async-done(((bf16[1040,128]{1,0:T(8,128)(2,1)}), bf16[4160,128]{1,0:T(8,128)(2,1)}) %all-gather.6.cloned.1.call-update) | async-done | bytes 1064976 | tf_op jit(solution)/shard_map/all_gather | solution.py:32
  33.9 0.8 convert_reduce_fusion
  34.7 1.2 fusion.53
  36.0 2.0 %multiply_reduce_fusion = (f32[256,16]{0,1:T(8,128)S(1)}, f32[256,16,64]{0,2,1:T(8,128)S(1)}) fusion(f32[256]{0:T(256)S(1)} %get-tuple-element.8, f32[256,16,64]{0,2,1:T(8,128)} %fusion.19, bf16[256,128]{1,0:T(8,128)(2,1)S(1)} %copy-done.5, bf16[16,64,128]{2,1,0:T(8,128)(2,1)S(1)} %bitcast.113, bf16[16,64,128]{2,1,0:T(8,128)(2,1)S(1)} %bitcast.114, ...), kind=kOutput, calls=%fused_computation.34 | convolution fusion | flops 405008384 | bytes 2983104 | tf_op jit(solution)/shard_map/hpn,tn->thp/dot_general | solution.py:287
  38.0 0.2 multiply_convert_fusion
  38.3 5.8 %fusion.56.partial_ref = f32[256,4096]{1,0:T(8,128)S(1)} fusion(bf16[256,1024]{0,1:T(8,128)(2,1)S(1)} %bitcast.106, bf16[1024,4096]{1,0:T(8,128)(2,1)} %param.21), kind=kOutput, calls=%fused_computation.94 | convolution fusion | flops 2147483648 | bytes 13107200 | tf_op jit(solution)/shard_map/dot_general | solution.py:294
  44.1 62.7 %shard_map.140 = (bf16[256,1024]{1,0:T(8,128)(2,1)S(1)}, bf16[256,4096]{1,0:T(8,128)(2,1)S(1)}) custom-call(f32[256,4096]{1,0:T(8,128)S(1)} %fusion.56.partial_ref, bf16[256,1024]{1,0:T(8,128)(2,1)S(1)} %copy-done.2, f32[1,4096]{1,0:T(1,128)S(1)} %bitcast.104), custom_call_target="tpu_custom_call" | custom-call | tf_op jit(solution)/shard_map/pallas_call | solution.py:223
  106.8 0.9 convolution_convert_fusion.2
  107.7 0.9 convolution_convert_fusion.3
  108.7 0.7 pad_maximum_fusion
  109.5 0.2 fusion.29
  109.7 7.1 %convolution_convert_fusion = bf16[256,1024]{1,0:T(8,128)(2,1)} fusion(bf16[256,4096]{1,0:T(8,128)(2,1)} %copy-done.1, bf16[4096,1024]{1,0:T(8,128)(2,1)} %param.23), kind=kOutput, calls=%fused_computation.25 | convolution fusion | flops 2147745792 | bytes 11010048 | tf_op jit(solution)/shard_map/dot_general | solution.py:298
  116.8 1.4 reshape.232
  118.2 6.5 %all-gather.4.cloned.1.call-done = bf16[1024,512]{0,1:T(8,128)(2,1)} async-done(((bf16[256,512]{0,1:T(8,128)(2,1)}), bf16[1024,512]{0,1:T(8,128)(2,1)}) %all-gather.4.cloned.1.call-update) | async-done | bytes 1048592 | tf_op jit(solution)/shard_map/all_gather | solution.py:308
  124.8 1.3 fusion.54
  126.1 1.6 %fusion = (f32[256,2,4]{0,2,1:T(4,128)S(1)}, f32[2,1024,256,4]{2,1,3,0:T(8,128)S(1)}) fusion(pred[256,1024]{0,1:T(8,128)(4,1)S(1)} %fusion.29, bf16[1024,2,128,1]{0,2,3,1:T(8,128)(2,1)S(1)} %bitcast.109, bf16[256,2,4,128]{3,2,1,0:T(4,128)(2,1)S(1)} %reshape.232), kind=kOutput, calls=%fused_computation.2 | convolution fusion | flops 543160320 | bytes 9707520 | tf_op jit(solution)/shard_map/tkgd,rkd->tkgr/dot_general | solution.py:316
  127.7 2.0 %fusion.1 = f32[256,2,4]{0,2,1:T(4,128)S(1)} fusion(f32[2,1024,256,4]{2,1,3,0:T(8,128)S(1)} %get-tuple-element.26, f32[256,2,4]{0,2,1:T(4,128)S(1)} %broadcast_maximum_fusion, pred[256,1024]{0,1:T(8,128)(4,1)S(1)} %fusion.29), kind=kLoop, calls=%fused_computation.3 | loop fusion | flops 10483712 | bytes 8667136 | tf_op jit(solution)/shard_map/reduce_sum | solution.py:327
  129.7 3.2 %fusion.10 = f32[2,128,256,4]{2,1,3,0:T(8,128)} fusion(bf16[1024,2,128,1]{0,2,3,1:T(8,128)(2,1)S(1)} %bitcast.117, f32[2,1024,256,4]{2,1,3,0:T(8,128)S(1)} %get-tuple-element.26, f32[256,2,4]{0,2,1:T(4,128)S(1)} %broadcast_maximum_fusion, pred[256,1024]{0,1:T(8,128)(4,1)S(1)} %fusion.29), kind=kOutput, calls=%fused_computation.12 | convolution fusion | flops 547356672 | bytes 10231808 | tf_op jit(solution)/shard_map/tkgr,rkd->tkgd/dot_general | solution.py:328
  132.9 2.6 %copy.63 = f32[256,1024]{1,0:T(8,128)} copy(f32[256,1024]{0,1:T(8,128)} %bitcast.110) | data formatting | bytes 2097152 | tf_op jit(solution)/shard_map/reshape | solution.py:334
  135.7 0.3 div.19
  136.0 2.3 %fusion.26 = bf16[256,1024]{1,0:T(8,128)(2,1)} fusion(f32[256,1024]{1,0:T(8,128)} %copy.63, f32[32,8,8,128]{3,2,1,0:T(8,128)S(1)} %bitcast.105, f32[256]{0:T(256)S(1)} %get-tuple-element.8), kind=kLoop, calls=%fused_computation.31 | loop fusion | flops 786432 | bytes 2622464 | tf_op jit(solution)/shard_map/convert_element_type | solution.py:341
  138.3 0.8 copy.88
  (40 shorter events, 1.0 us)
Async XLA Ops:
  7.2 99.6 %copy-start = (bf16[4096,256]{1,0:T(8,128)(2,1)S(1)}, bf16[4096,256]{1,0:T(8,128)(2,1)}, u32[]{:S(2)}) copy-start(bf16[4096,256]{1,0:T(8,128)(2,1)} %param.25) | copy-start | bytes 6291460
  7.2 26.7 %all-gather.6.cloned.1.call-start = ((), (), s32[]{:S(2)}) async-start(), calls=%async_computation.1 | async-start | bytes 1331200 | tf_op jit(solution)/shard_map/all_gather | solution.py:32
  14.2 110.6 %all-gather.4.cloned.1.call-start = ((), (), s32[]{:S(2)}) async-start(), calls=%async_computation | async-start | bytes 1310720 | tf_op jit(solution)/shard_map/all_gather | solution.py:308
  16.1 19.9 %copy-start.5 = (bf16[256,128]{1,0:T(8,128)(2,1)S(1)}, bf16[256,128]{1,0:T(8,128)(2,1)}, u32[]{:S(2)}) copy-start(bf16[256,128]{1,0:T(8,128)(2,1)} %param.17) | copy-start | bytes 196612
  38.2 5.9 %copy-start.2 = (bf16[256,1024]{1,0:T(8,128)(2,1)S(1)}, bf16[256,1024]{1,0:T(8,128)(2,1)}, u32[]{:S(2)}) copy-start(bf16[256,1024]{1,0:T(8,128)(2,1)} %residual_ref.1) | copy-start | bytes 1572868
  38.2 5.8 %copy-start.3 = (f32[4096]{0:T(1024)S(1)}, f32[4096]{0:T(1024)}, u32[]{:S(2)}) copy-start(f32[4096]{0:T(1024)} %param.22) | copy-start | bytes 49156
  44.1 63.6 %copy-start.4 = (bf16[4096,256]{1,0:T(8,128)(2,1)S(1)}, bf16[4096,256]{1,0:T(8,128)(2,1)}, u32[]{:S(2)}) copy-start(bf16[4096,256]{1,0:T(8,128)(2,1)} %param.24) | copy-start | bytes 6291460
  106.8 1.9 %copy-start.1 = (bf16[256,4096]{1,0:T(8,128)(2,1)}, bf16[256,4096]{1,0:T(8,128)(2,1)S(1)}, u32[]{:S(2)}) copy-start(bf16[256,4096]{1,0:T(8,128)(2,1)S(1)} %get-tuple-element.5) | copy-start | bytes 6291460
Sparse Core Ops, SparseCore 0:
  14.3 19.5 all-gather.5
  109.6 15.1 all-gather.3

commit v3 on v2

--- a/solution.py
+++ b/solution.py
@@ -216,7 +216,7 @@
 
 def line_sum_and_gather(partial_value, residual, norm_gain, count):
     rows, width = residual.shape
-    chunks = 4 if rows % 64 == 0 else 1
+    chunks = 8 if rows % 128 == 0 else 1
     steps = count - 1
     piece = rows // chunks
     messages = (2, chunks, steps)
@@ -242,6 +242,56 @@
             collective_id=0, has_side_effects=True, vmem_limit_bytes=40 * 1024 * 1024
         ),
     )(partial_value, residual, norm_gain.reshape(1, width * count))
+
+
+def attention_kernel(group_size, limits_ref, query_ref, key_ref, value_ref, out_ref):
+    rows, count = query_ref.shape[0], key_ref.shape[0]
+    limit, first = limits_ref[0], limits_ref[1]
+    key_pos = lax.broadcasted_iota(jnp.int32, (rows, count), 1)
+    positions = first + lax.broadcasted_iota(jnp.int32, (rows, count), 0)
+    allowed = (key_pos <= positions) & (key_pos < limit)
+    live = first + lax.broadcasted_iota(jnp.int32, (rows, 1), 0) < limit
+    for head in range(group_size):
+        columns = slice(head * HEAD_DIM, (head + 1) * HEAD_DIM)
+        scores = lax.dot_general(
+            query_ref[:, columns],
+            key_ref[...],
+            (((1,), (1,)), ((), ())),
+            preferred_element_type=jnp.float32,
+        ) * HEAD_DIM ** (-0.5)
+        masked = jnp.where(allowed, scores, NEG_BIG)
+        weights = jnp.exp(masked - jnp.max(masked, axis=1, keepdims=True))
+        total = jnp.sum(weights, axis=1, keepdims=True)
+        accum = jnp.dot(
+            weights.astype(jnp.bfloat16), value_ref[...], preferred_element_type=jnp.float32
+        )
+        head_out = jnp.where(live, accum / jnp.where(live, total, 1.0), 0.0)
+        out_ref[:, columns] = head_out.astype(jnp.bfloat16)
+
+
+def attention(queries, key_value, limit, first):
+    rows, count = queries.shape[0], key_value.shape[0]
+    kv_local = key_value.shape[1] // (2 * HEAD_DIM)
+    group_size = queries.shape[1] // (kv_local * HEAD_DIM)
+    wide = (rows, group_size * HEAD_DIM)
+    return pl.pallas_call(
+        functools.partial(attention_kernel, group_size),
+        grid=(kv_local,),
+        out_shape=jax.ShapeDtypeStruct(queries.shape, jnp.bfloat16),
+        in_specs=[
+            pl.BlockSpec(memory_space=pltpu.SMEM),
+            pl.BlockSpec(wide, lambda head: (0, head)),
+            pl.BlockSpec((count, HEAD_DIM), lambda head: (0, head)),
+            pl.BlockSpec((count, HEAD_DIM), lambda head: (0, head + kv_local)),
+        ],
+        out_specs=pl.BlockSpec(wide, lambda head: (0, head)),
+        compiler_params=pltpu.CompilerParams(vmem_limit_bytes=40 * 1024 * 1024),
+        cost_estimate=pl.CostEstimate(
+            flops=4 * rows * count * queries.shape[1],
+            bytes_accessed=4 * queries.size + 2 * key_value.size,
+            transcendentals=rows * count * kv_local * group_size,
+        ),
+    )(jnp.stack([limit, first]), queries, key_value, key_value)
 
 
 def body(
@@ -300,47 +350,10 @@
     )
     keys = jnp.dot(attn_in, key_weight, preferred_element_type=jnp.float32).astype(jnp.bfloat16)
     values = jnp.dot(attn_in, value_weight, preferred_element_type=jnp.float32).astype(jnp.bfloat16)
-    query_local = query_weight.shape[1] // HEAD_DIM
-    kv_local = key_weight.shape[1] // HEAD_DIM
-    group_size = query_local // kv_local
-    grouped = queries.reshape(rows, kv_local, group_size, HEAD_DIM)
-    best = jnp.full((rows, query_local), NEG_BIG, jnp.float32)
     key_value = lax.all_gather(
         jnp.concatenate([keys, values], axis=1), "seq", axis=0, tiled=True
     )
-    key_piece = key_value[:, : keys.shape[1]]
-    value_piece = key_value[:, keys.shape[1] :]
-    count = key_piece.shape[0]
-    key_pos = jnp.arange(count, dtype=jnp.int32)
-    allowed = (key_pos[None, :] <= positions[:, None]) & (key_pos[None, :] < limit)
-    scores = jnp.einsum(
-        "tkgd,rkd->tkgr",
-        grouped,
-        key_piece.reshape(count, kv_local, HEAD_DIM),
-        preferred_element_type=jnp.float32,
-    ) * HEAD_DIM ** (-0.5)
-    scores = scores.reshape(rows, query_local, count)
-    allowed_wide = allowed[:, None, :]
-    masked = jnp.where(allowed_wide, scores, NEG_BIG)
-    new_best = jnp.maximum(best, jnp.max(masked, axis=2))
-    weights = jnp.where(allowed_wide, jnp.exp(masked - new_best[:, :, None]), 0.0)
-    total = jnp.sum(weights, axis=2)
-    update = jnp.einsum(
-        "tkgr,rkd->tkgd",
-        weights.astype(jnp.bfloat16).reshape(rows, kv_local, group_size, count),
-        value_piece.reshape(count, kv_local, HEAD_DIM),
-        preferred_element_type=jnp.float32,
-    )
-    accum = update.reshape(rows, query_local, HEAD_DIM)
-    folded = (new_best, total, accum)
-    total = folded[1]
-    accum = folded[2]
-    safe_total = jnp.where(live_rows[:, None], total, 1.0)
-    head_out = (
-        (accum / safe_total[:, :, None] * live[:, None, None])
-        .astype(jnp.bfloat16)
-        .reshape(rows, query_local * HEAD_DIM)
-    )
+    head_out = attention(queries, key_value, limit, seq_index * rows)
     return (layer_out, head_out)
 
 

time: 147 us -> 142 us (0.966)
  Pallas kernels: 62.7 us -> 70.2 us
  matrix products: 28.6 us -> 22.7 us
  local copies, waits for them, and re-layouts: 10.2 us -> 5.66 us
  other arithmetic: 9.43 us -> 4.98 us
  waiting for transfers between devices: 19.9 us -> 22.6 us
    pallas_call x0 -> x1, Pallas kernels: none -> 5.93 us  [attention(): pl.pallas_call(functools.partial(attention_kernel, group_size), grid=(kv_...]
    dot_general x2 -> x0, matrix products: 4.81 us -> none  [the longest x1 3.23 us: body(): jnp.einsum('tkgr,rkd->tkgd', weights.astype(jnp.bfloat16).reshape(rows, k...]
    reshape x3 -> x1, local copies, waits for them, and re-layouts: 4 us -> 0.01 us  [the longest x1 2.59 us: body(): accum = update.reshape(rows, query_local, HEAD_DIM)]
    all_gather x1, waiting for transfers between devices: 6.55 us -> 9.27 us  [body(): lax.all_gather(jnp.concatenate([keys, values], axis=1), 'seq', axis=0, ti...]
    convert_element_type x1 -> x0, other arithmetic: 2.26 us -> none  [body(): head_out = (accum / safe_total[:, :, None] * live[:, None, None]).astype(...]
    reduce_sum x1 -> x0, other arithmetic: 2.03 us -> none  [body(): total = jnp.sum(weights, axis=2)]
    pallas_call x1, Pallas kernels: 62.7 us -> 64.3 us  [line_sum_and_gather(): pl.pallas_call(functools.partial(line_kernel, count, chunks), out_shape=(...]
    unnamed x16 -> x18, local copies, waits for them, and re-layouts: 2.26 us -> 3.48 us
  transfers between devices with their start and end apart: 2 -> 2, of which waited for: 2 -> 2; matrix products, arithmetic and copies ran while one was open for 10% -> 9% of each run, Pallas kernels for 0% -> 0%
where the time goes in v3:
time: 142 us; the launch traced here: 141 us
  Pallas kernels  70.2 us (49%)
  matrix products  22.7 us (16%)
  waiting for transfers between devices  22.6 us (16%)
  between operations  15 us (11%)
  local copies, waits for them, and re-layouts  5.66 us (4%)
  other arithmetic  4.98 us (4%)
    pallas_call x1, Pallas kernels, line_sum_and_gather(): pl.pallas_call(functools.partial(line_kernel, count, chunks), out_shape=(...  64.3 us
    all_gather x1, waiting for transfers between devices, incoming_state(): pieces = lax.all_gather(packed, axis)  13.3 us
    all_gather x1, waiting for transfers between devices, body(): lax.all_gather(jnp.concatenate([keys, values], axis=1), 'seq', axis=0, ti...  9.27 us
    dot_general x1, matrix products, body(): jnp.dot(attn_in, query_weight, preferred_element_type=jnp.float32)  6.34 us
    dot_general x1, matrix products, body(): jnp.dot(normed, out_weight, preferred_element_type=jnp.float32)  5.95 us
    pallas_call x1, Pallas kernels, attention(): pl.pallas_call(functools.partial(attention_kernel, group_size), grid=(kv_...  5.93 us
    dot_general x1, matrix products, body(): within = jnp.einsum('hts,shp->thp', mixing, inputs, precision=HIGHEST)  4.42 us
    unnamed x18, local copies, waits for them, and re-layouts  3.48 us
  transfers between devices with their start and end apart: 2, of which 2 were waited for; matrix products, arithmetic and copies ran while one was open for 9% of the time, Pallas kernels for 0%

profile of v3, /device:TPU:0, one launch (start us, length us, event | category | flops | bytes accessed | tf_op | source)
XLA Modules:
  0.0 141.3 jit_solution(20873379630526356)
XLA Ops:
  8.0 0.7 neg.8
  8.7 0.8 multiply_bitcast_fusion.1
  9.5 0.6 reduce-window.6
  10.0 0.2 slice_reduce_fusion
  10.2 0.1 copy_bitcast_fusion
  10.3 0.1 slice.42
  10.4 0.1 copy.52
  10.5 0.1 copy.53
  10.6 1.2 copy.45
  11.9 0.1 exponential_bitcast_fusion
  12.0 1.5 %convolution_convert_fusion.1 = bf16[16,64,128]{2,1,0:T(8,128)(2,1)S(1)} fusion(bf16[256,16,64]{0,2,1:T(8,128)(2,1)S(1)} %bitcast.71, f32[256,16]{0,1:T(8,128)S(1)} %get-tuple-element.12, bf16[256,128]{1,0:T(8,128)(2,1)} %param.16), kind=kOutput, calls=%fused_computation.19 | convolution fusion | flops 403308544 | bytes 868352 | tf_op jit(solution)/shard_map/hs,shp,sn->hpn/dot_general | solution.py:333
  13.5 0.7 fusion.27
  14.3 0.8 mul.135
  15.1 1.1 fusion.39
  16.1 4.4 %fusion.13 = f32[256,16,64]{0,2,1:T(8,128)} fusion(bf16[256,16,64]{0,2,1:T(8,128)(2,1)S(1)} %bitcast.72, f32[16,256]{1,0:T(8,128)S(1)} %get-tuple-element.7, f32[256,256]{1,0:T(8,128)S(1)} %fusion.39, f32[16,256]{1,0:T(8,128)S(1)} %copy_bitcast_fusion, pred[256,256]{1,0:T(8,128)(4,1)S(1)} %iota_compare_fusion.1), kind=kOutput, calls=%fused_computation.14 | convolution fusion | flops 810549248 | bytes 1933312 | tf_op jit(solution)/shard_map/hts,shp->thp/dot_general | solution.py:331
  20.6 13.3 %all-gather.6.cloned.1.call-done = bf16[4160,128]{1,0:T(8,128)(2,1)} async-done(((bf16[1040,128]{1,0:T(8,128)(2,1)}), bf16[4160,128]{1,0:T(8,128)(2,1)}) %all-gather.6.cloned.1.call-update) | async-done | bytes 1064976 | tf_op jit(solution)/shard_map/all_gather | solution.py:32
  33.9 0.8 convert_reduce_fusion
  34.7 1.2 fusion.38
  35.9 0.1 select_reduce_fusion
  36.0 2.0 %multiply_reduce_fusion = (f32[256,16]{0,1:T(8,128)S(1)}, f32[256,16,64]{0,2,1:T(8,128)S(1)}) fusion(f32[256]{0:T(256)S(1)} %compare_convert_fusion, f32[256,16,64]{0,2,1:T(8,128)} %fusion.13, bf16[256,128]{1,0:T(8,128)(2,1)S(1)} %copy-done.5, bf16[16,64,128]{2,1,0:T(8,128)(2,1)S(1)} %bitcast.75, bf16[16,64,128]{2,1,0:T(8,128)(2,1)S(1)} %bitcast.76, ...), kind=kOutput, calls=%fused_computation.23 | convolution fusion | flops 405008384 | bytes 2983104 | tf_op jit(solution)/shard_map/hpn,tn->thp/dot_general | solution.py:337
  38.0 0.2 multiply_convert_fusion
  38.3 6.0 %fusion.40.partial_ref = f32[256,4096]{1,0:T(8,128)S(1)} fusion(bf16[256,1024]{0,1:T(8,128)(2,1)S(1)} %bitcast.70, bf16[1024,4096]{1,0:T(8,128)(2,1)} %param.21), kind=kOutput, calls=%fused_computation.72 | convolution fusion | flops 2147483648 | bytes 13107200 | tf_op jit(solution)/shard_map/dot_general | solution.py:344
  44.3 64.3 %shard_map.140 = (bf16[256,1024]{1,0:T(8,128)(2,1)S(1)}, bf16[256,4096]{1,0:T(8,128)(2,1)S(1)}) custom-call(f32[256,4096]{1,0:T(8,128)S(1)} %fusion.40.partial_ref, bf16[256,1024]{1,0:T(8,128)(2,1)S(1)} %copy-done.1, f32[1,4096]{1,0:T(1,128)S(1)} %bitcast.69), custom_call_target="tpu_custom_call" | custom-call | tf_op jit(solution)/shard_map/pallas_call | solution.py:223
  108.6 0.7 convolution_convert_fusion.2
  109.3 0.7 convolution_convert_fusion.3
  110.1 0.7 pad_maximum_fusion
  110.8 0.1 pad_add_fusion.limits_ref
  110.9 6.3 %convolution_convert_fusion.query_ref = bf16[256,1024]{1,0:T(8,128)(2,1)S(1)} fusion(bf16[256,4096]{1,0:T(8,128)(2,1)} %copy-done.3, bf16[4096,1024]{1,0:T(8,128)(2,1)} %param.23), kind=kOutput, calls=%fused_computation.18 | convolution fusion | flops 2147745792 | bytes 11010048 | tf_op jit(solution)/shard_map/dot_general | solution.py:348
  117.2 9.3 %all-gather.4.cloned.1.call-done.key_ref.value_ref = bf16[1024,512]{1,0:T(8,128)(2,1)} async-done(((bf16[256,512]{1,0:T(8,128)(2,1)}), bf16[1024,512]{1,0:T(8,128)(2,1)}) %all-gather.4.cloned.1.call-update) | async-done | bytes 1048592 | tf_op jit(solution)/shard_map/all_gather | solution.py:353
  126.5 1.2 copy-done.4
  127.7 5.9 %shard_map.141 = bf16[256,1024]{1,0:T(8,128)(2,1)} custom-call(s32[2]{0:T(128)S(1)} %pad_add_fusion.limits_ref, bf16[256,1024]{1,0:T(8,128)(2,1)S(1)} %convolution_convert_fusion.query_ref, bf16[1024,512]{1,0:T(8,128)(2,1)S(1)} %copy-done.4, bf16[1024,512]{1,0:T(8,128)(2,1)S(1)} %copy-done.4), custom_call_target="tpu_custom_call" | custom-call | flops 1073741824 | bytes 2097152 | tf_op jit(solution)/shard_map/pallas_call | solution.py:277
  133.7 0.8 copy.65
  (29 shorter events, 0.4 us)
Async XLA Ops:
  7.2 101.4 %copy-start = (bf16[4096,256]{1,0:T(8,128)(2,1)S(1)}, bf16[4096,256]{1,0:T(8,128)(2,1)}, u32[]{:S(2)}) copy-start(bf16[4096,256]{1,0:T(8,128)(2,1)} %param.25) | copy-start | bytes 6291460
  7.2 26.7 %all-gather.6.cloned.1.call-start = ((), (), s32[]{:S(2)}) async-start(), calls=%async_computation.1 | async-start | bytes 1331200 | tf_op jit(solution)/shard_map/all_gather | solution.py:32
  14.2 112.3 %all-gather.4.cloned.1.call-start = ((), (), s32[]{:S(2)}) async-start(), calls=%async_computation | async-start | bytes 1310720 | tf_op jit(solution)/shard_map/all_gather | solution.py:353
  16.1 19.9 %copy-start.5 = (bf16[256,128]{1,0:T(8,128)(2,1)S(1)}, bf16[256,128]{1,0:T(8,128)(2,1)}, u32[]{:S(2)}) copy-start(bf16[256,128]{1,0:T(8,128)(2,1)} %param.17) | copy-start | bytes 196612
  38.3 6.0 %copy-start.1 = (bf16[256,1024]{1,0:T(8,128)(2,1)S(1)}, bf16[256,1024]{1,0:T(8,128)(2,1)}, u32[]{:S(2)}) copy-start(bf16[256,1024]{1,0:T(8,128)(2,1)} %residual_ref.1) | copy-start | bytes 1572868
  38.3 6.0 %copy-start.2 = (f32[4096]{0:T(1024)S(1)}, f32[4096]{0:T(1024)}, u32[]{:S(2)}) copy-start(f32[4096]{0:T(1024)} %param.22) | copy-start | bytes 49156
  44.3 65.1 %copy-start.6 = (bf16[4096,256]{1,0:T(8,128)(2,1)S(1)}, bf16[4096,256]{1,0:T(8,128)(2,1)}, u32[]{:S(2)}) copy-start(bf16[4096,256]{1,0:T(8,128)(2,1)} %param.24) | copy-start | bytes 6291460
  108.6 1.5 %copy-start.3 = (bf16[256,4096]{1,0:T(8,128)(2,1)}, bf16[256,4096]{1,0:T(8,128)(2,1)S(1)}, u32[]{:S(2)}) copy-start(bf16[256,4096]{1,0:T(8,128)(2,1)S(1)} %get-tuple-element.5) | copy-start | bytes 6291460
  126.5 1.2 copy-start.4
Sparse Core Ops, SparseCore 0:
  14.3 19.5 all-gather.5
  110.9 15.5 all-gather.3

commit v4 on v3

--- a/solution.py
+++ b/solution.py
@@ -44,12 +44,20 @@
 
 def line_kernel(
     count,
+    shards,
     chunks,
     partial_ref,
     residual_ref,
     gain_ref,
+    query_weight_ref,
+    key_weight_ref,
+    value_weight_ref,
     layer_ref,
+    query_ref,
+    key_value_ref,
+    weight_ref,
     attn_ref,
+    shared_ref,
     stage_ref,
     landed_ref,
     gathered_ref,
@@ -58,6 +66,9 @@
     sum_recv,
     copy_send,
     copy_recv,
+    shard_send,
+    shard_recv,
+    weight_sem,
 ):
     mine = lax.axis_index("head")
     last = count - 1
@@ -65,6 +76,21 @@
     rows = residual_ref.shape[0] // chunks
     place = (mine, last - mine)
 
+    shard = lax.axis_index("seq")
+    query_width = query_ref.shape[1]
+    kv_width = key_weight_ref.shape[1]
+    starts = (0, kv_width, 2 * kv_width)
+    loads = [
+        pltpu.make_async_copy(
+            source, weight_ref.at[:, pl.ds(start, source.shape[1])], weight_sem.at[index]
+        )
+        for index, (source, start) in enumerate(
+            zip((key_weight_ref, value_weight_ref, query_weight_ref), starts)
+        )
+    ]
+    for load in loads:
+        load.start()
+
     barrier = pltpu.get_barrier_semaphore()
 
     def greet(neighbour):
@@ -80,13 +106,27 @@
     def _():
         greet(mine + 1)
 
+    for offset in range(1, shards):
+        other = (shard + offset) % shards
+        pl.semaphore_signal(
+            barrier, inc=1, device_id={"seq": other}, device_id_type=pl.DeviceIdType.MESH
+        )
+
     @pl.when((mine == 0) | (mine == last))
     def _():
-        pl.semaphore_wait(barrier, 1)
+        pl.semaphore_wait(barrier, shards)
 
     @pl.when((mine > 0) & (mine < last))
     def _():
-        pl.semaphore_wait(barrier, 2)
+        pl.semaphore_wait(barrier, shards + 1)
+
+    for other in range(shards):
+
+        @pl.when(other > shard)
+        def _():
+            shared_ref[pl.ds(other * residual_ref.shape[0], residual_ref.shape[0])] = jnp.zeros(
+                (residual_ref.shape[0], 2 * kv_width), jnp.bfloat16
+            )
 
     def neighbour(way):
         return mine + 1 if way == 0 else mine - 1
@@ -114,6 +154,48 @@
             device_id={"head": neighbour(way)},
             device_id_type=pl.DeviceIdType.MESH,
         )
+
+    def shard_copy(chunk, offset, source):
+        start = pl.multiple_of(source * residual_ref.shape[0] + chunk * rows, 16)
+        block = shared_ref.at[pl.ds(start, rows)]
+        return pltpu.make_async_remote_copy(
+            src_ref=block,
+            dst_ref=block,
+            send_sem=shard_send.at[chunk, offset],
+            recv_sem=shard_recv.at[chunk, offset],
+            device_id={"seq": (shard + offset) % shards},
+            device_id_type=pl.DeviceIdType.MESH,
+        )
+
+    def project(chunk):
+        here = pl.ds(chunk * rows, rows)
+        there = pl.ds(pl.multiple_of(shard * residual_ref.shape[0] + chunk * rows, 16), rows)
+
+        def product(tile):
+            columns = pl.ds(pl.multiple_of(tile * kv_width, 128), kv_width)
+            return jnp.dot(
+                attn_ref[here], weight_ref[:, columns], preferred_element_type=jnp.float32
+            ).astype(jnp.bfloat16)
+
+        if chunk == 0:
+            for load in loads:
+                load.wait()
+
+        @pl.loop(0, 2)
+        def _(tile):
+            columns = pl.ds(pl.multiple_of(tile * kv_width, 128), kv_width)
+            shared_ref[there, columns] = product(tile)
+
+        for offset in range(1, shards):
+
+            @pl.when(shard + offset < shards)
+            def _():
+                shard_copy(chunk, offset, shard).start()
+
+        @pl.loop(0, query_width // kv_width)
+        def _(tile):
+            columns = pl.ds(pl.multiple_of(tile * kv_width, 128), kv_width)
+            query_ref[here, columns] = product(tile + 2)
 
     def own_part(chunk, owner):
         columns = pl.ds(pl.multiple_of(owner * width, 128), width)
@@ -198,8 +280,9 @@
                 finish_sum(chunk)
             elif last < stage < 2 * last:
                 forward(chunk, stage - last)
-            elif stage == 2 * last:
-                normalise(chunk)
+        if 0 <= tick - 2 * last < chunks:
+            normalise(tick - 2 * last)
+            project(tick - 2 * last)
 
     for chunk in range(chunks):
         for step in range(last):
@@ -213,22 +296,40 @@
                 def _():
                     block_copy(way, chunk, step, real(way, place[way] - step)).wait_send()
 
-
-def line_sum_and_gather(partial_value, residual, norm_gain, count):
+        for offset in range(1, shards):
+
+            @pl.when(shard + offset < shards)
+            def _():
+                shard_copy(chunk, offset, shard).wait_send()
+
+            @pl.when(shard >= offset)
+            def _():
+                shard_copy(chunk, offset, shard - offset).wait_recv()
+
+    key_value_ref[...] = shared_ref[...]
+
+
+def line_layer(partial_value, residual, norm_gain, weights, count, shards):
     rows, width = residual.shape
-    chunks = 8 if rows % 128 == 0 else 1
-    steps = count - 1
+    model_width = width * count
+    query_width, kv_width = weights[0].shape[1], weights[1].shape[1]
+    chunks = 4 if rows % 64 == 0 else 1
     piece = rows // chunks
-    messages = (2, chunks, steps)
+    messages = (2, chunks, count - 1)
+    vmem = pl.BlockSpec(memory_space=pltpu.VMEM)
     return pl.pallas_call(
-        functools.partial(line_kernel, count, chunks),
+        functools.partial(line_kernel, count, shards, chunks),
         out_shape=(
             jax.ShapeDtypeStruct((rows, width), jnp.bfloat16),
-            jax.ShapeDtypeStruct((rows, width * count), jnp.bfloat16),
+            jax.ShapeDtypeStruct((rows, query_width), jnp.bfloat16),
+            jax.ShapeDtypeStruct((shards * rows, 2 * kv_width), jnp.bfloat16),
         ),
-        in_specs=[pl.BlockSpec(memory_space=pltpu.VMEM)] * 3,
-        out_specs=[pl.BlockSpec(memory_space=pltpu.VMEM)] * 2,
+        in_specs=[vmem] * 3 + [pl.BlockSpec(memory_space=pltpu.HBM)] * 3,
+        out_specs=[vmem] * 3,
         scratch_shapes=[
+            pltpu.VMEM((model_width, 2 * kv_width + query_width), jnp.bfloat16),
+            pltpu.VMEM((rows, model_width), jnp.bfloat16),
+            pltpu.VMEM((shards * rows, 2 * kv_width), jnp.bfloat16),
             pltpu.VMEM(messages + (piece, width), jnp.bfloat16),
             pltpu.VMEM(messages + (piece, width), jnp.bfloat16),
             pltpu.VMEM((count, rows, width), jnp.bfloat16),
@@ -237,11 +338,14 @@
             pltpu.SemaphoreType.DMA(messages),
             pltpu.SemaphoreType.DMA(messages),
             pltpu.SemaphoreType.DMA(messages),
+            pltpu.SemaphoreType.DMA((chunks, shards)),
+            pltpu.SemaphoreType.DMA((chunks, shards)),
+            pltpu.SemaphoreType.DMA((3,)),
         ],
         compiler_params=pltpu.CompilerParams(
-            collective_id=0, has_side_effects=True, vmem_limit_bytes=40 * 1024 * 1024
+            collective_id=0, has_side_effects=True, vmem_limit_bytes=52 * 1024 * 1024
         ),
-    )(partial_value, residual, norm_gain.reshape(1, width * count))
+    )(partial_value, residual, norm_gain.reshape(1, model_width), *weights)
 
 
 def attention_kernel(group_size, limits_ref, query_ref, key_ref, value_ref, out_ref):
@@ -342,16 +446,13 @@
     ).astype(jnp.bfloat16)
     normed = normed.reshape(rows, local_heads * head_width)
     partial_value = jnp.dot(normed, out_weight, preferred_element_type=jnp.float32)
-    layer_out, attn_in = line_sum_and_gather(
-        partial_value, residual, norm_gain, lax.axis_size("head")
-    )
-    queries = jnp.dot(attn_in, query_weight, preferred_element_type=jnp.float32).astype(
-        jnp.bfloat16
-    )
-    keys = jnp.dot(attn_in, key_weight, preferred_element_type=jnp.float32).astype(jnp.bfloat16)
-    values = jnp.dot(attn_in, value_weight, preferred_element_type=jnp.float32).astype(jnp.bfloat16)
-    key_value = lax.all_gather(
-        jnp.concatenate([keys, values], axis=1), "seq", axis=0, tiled=True
+    layer_out, queries, key_value = line_layer(
+        partial_value,
+        residual,
+        norm_gain,
+        (query_weight, key_weight, value_weight),
+        lax.axis_size("head"),
+        lax.axis_size("seq"),
     )
     head_out = attention(queries, key_value, limit, seq_index * rows)
     return (layer_out, head_out)

time: 142 us -> 131 us (0.923)
  matrix products: 22.7 us -> 14.4 us
  waiting for transfers between devices: 22.6 us -> 14.4 us
  Pallas kernels: 70.2 us -> 77.4 us
    all_gather x1 -> x0, waiting for transfers between devices: 9.27 us -> none  [body(): lax.all_gather(jnp.concatenate([keys, values], axis=1), 'seq', axis=0, ti...]
    dot_general x3 -> x0, matrix products: 7.78 us -> none  [the longest x1 6.34 us: body(): jnp.dot(attn_in, query_weight, preferred_element_type=jnp.float32)]
    pallas_call x1, Pallas kernels: 64.3 us -> 71.5 us  [line_layer(): pl.pallas_call(functools.partial(line_kernel, count, shards, chunks), out...]
    dot_general x1, matrix products: 5.95 us -> 7.74 us  [body(): jnp.dot(normed, out_weight, preferred_element_type=jnp.float32)]
    unnamed x18 -> x12, local copies, waits for them, and re-layouts: 3.48 us -> 3.46 us
  transfers between devices with their start and end apart: 2 -> 1, of which waited for: 2 -> 1; matrix products, arithmetic and copies ran while one was open for 9% -> 4% of each run, Pallas kernels for 0% -> 0%
where the time goes in v4:
time: 131 us
  Pallas kernels  77.4 us (59%)
  between operations  14.8 us (11%)
  matrix products  14.4 us (11%)
  waiting for transfers between devices  14.4 us (11%)
  local copies, waits for them, and re-layouts  5.63 us (4%)
  other arithmetic  4.26 us (3%)
    pallas_call x1, Pallas kernels, line_layer(): pl.pallas_call(functools.partial(line_kernel, count, shards, chunks), out...  71.5 us
    all_gather x1, waiting for transfers between devices, incoming_state(): pieces = lax.all_gather(packed, axis)  14.4 us
    dot_general x1, matrix products, body(): jnp.dot(normed, out_weight, preferred_element_type=jnp.float32)  7.74 us
    pallas_call x1, Pallas kernels, attention(): pl.pallas_call(functools.partial(attention_kernel, group_size), grid=(kv_...  5.94 us
    unnamed x12, local copies, waits for them, and re-layouts  3.46 us
    dot_general x1, matrix products, body(): within = jnp.einsum('hts,shp->thp', mixing, inputs, precision=HIGHEST)  3.38 us
  transfers between devices with their start and end apart: 1, of which 1 were waited for; matrix products, arithmetic and copies ran while one was open for 4% of the time, Pallas kernels for 0%

profile of v4, /device:TPU:0, one launch (start us, length us, event | category | flops | bytes accessed | tf_op | source)
XLA Modules:
  0.0 131.0 jit_solution(13585491348795092850)
XLA Ops:
  7.2 0.0 copy-start
  7.2 0.0 all-gather.3.cloned.1.call-start
  7.9 0.7 neg.8
  8.5 0.8 multiply_bitcast_fusion.1
  9.3 0.6 reduce-window.6
  9.9 0.2 slice_reduce_fusion
  10.1 0.1 copy_bitcast_fusion
  10.2 0.1 slice.42
  10.3 0.1 copy.40
  10.4 0.1 copy.41
  10.5 1.2 copy.37
  11.7 0.1 exponential_bitcast_fusion
  11.8 1.5 %convolution_convert_fusion = bf16[16,64,128]{2,1,0:T(8,128)(2,1)S(1)} fusion(bf16[256,16,64]{0,2,1:T(8,128)(2,1)S(1)} %bitcast.65, f32[256,16]{0,1:T(8,128)S(1)} %get-tuple-element.14, bf16[256,128]{1,0:T(8,128)(2,1)} %param.16), kind=kOutput, calls=%fused_computation.18 | convolution fusion | flops 403308544 | bytes 868352 | tf_op jit(solution)/shard_map/hs,shp,sn->hpn/dot_general | solution.py:437
  13.3 0.7 fusion.27
  14.0 0.0 all-gather.3.cloned.1.call-update
  14.1 0.8 mul.135
  14.8 0.1 pad_add_fusion.limits_ref
  15.0 1.0 fusion.39
  16.0 3.4 %fusion.13 = f32[256,16,64]{0,2,1:T(8,128)S(1)} fusion(bf16[256,16,64]{0,2,1:T(8,128)(2,1)S(1)} %bitcast.66, f32[16,256]{1,0:T(8,128)S(1)} %get-tuple-element.9, f32[256,256]{1,0:T(8,128)S(1)} %fusion.39, f32[16,256]{1,0:T(8,128)S(1)} %copy_bitcast_fusion, pred[256,256]{1,0:T(8,128)(4,1)S(1)} %iota_compare_fusion.1), kind=kOutput, calls=%fused_computation.14 | convolution fusion | flops 810549248 | bytes 1933312 | tf_op jit(solution)/shard_map/hts,shp->thp/dot_general | solution.py:435
  19.4 14.4 %all-gather.3.cloned.1.call-done = bf16[4160,128]{1,0:T(8,128)(2,1)} async-done(((bf16[1040,128]{1,0:T(8,128)(2,1)}), bf16[4160,128]{1,0:T(8,128)(2,1)}) %all-gather.3.cloned.1.call-update) | async-done | bytes 1064976 | tf_op jit(solution)/shard_map/all_gather | solution.py:32
  33.7 0.8 convert_reduce_fusion
  34.6 1.2 fusion.38
  35.7 0.1 select_reduce_fusion
  35.8 0.1 exponential_select_fusion
  35.9 0.8 multiply_reduce_fusion
  36.7 0.2 multiply_convert_fusion
  36.9 0.0 copy-start.1
  36.9 7.7 %fusion.40.partial_ref = f32[256,4096]{1,0:T(8,128)} fusion(bf16[256,1024]{0,1:T(8,128)(2,1)S(1)} %bitcast.64, bf16[1024,4096]{1,0:T(8,128)(2,1)} %param.21), kind=kOutput, calls=%fused_computation.68 | convolution fusion | flops 2147483648 | bytes 13107200 | tf_op jit(solution)/shard_map/dot_general | solution.py:448
  44.7 71.5 %shard_map.140 = (bf16[256,1024]{1,0:T(8,128)(2,1)S(1)}, bf16[256,1024]{1,0:T(8,128)(2,1)S(1)}, bf16[1024,512]{1,0:T(8,128)(2,1)}) custom-call(f32[256,4096]{1,0:T(8,128)} %fusion.40.partial_ref, bf16[256,1024]{1,0:T(8,128)(2,1)S(1)} %copy-done.1, f32[1,4096]{1,0:T(1,128)S(1)} %bitcast.63, bf16[4096,1024]{1,0:T(8,128)(2,1)} %query_weight_ref.1, ...), custom_call_target="tpu_custom_call" | custom-call | tf_op jit(solution)/shard_map/pallas_call | solution.py:320
  116.2 1.2 copy-done.3
  117.4 5.9 %shard_map.141 = bf16[256,1024]{1,0:T(8,128)(2,1)} custom-call(s32[2]{0:T(128)S(1)} %pad_add_fusion.limits_ref, bf16[256,1024]{1,0:T(8,128)(2,1)S(1)} %get-tuple-element.6.query_ref, bf16[1024,512]{1,0:T(8,128)(2,1)S(1)} %copy-done.3, bf16[1024,512]{1,0:T(8,128)(2,1)S(1)} %copy-done.3), custom_call_target="tpu_custom_call" | custom-call | flops 1073741824 | bytes 2097152 | tf_op jit(solution)/shard_map/pallas_call | solution.py:381
  123.3 0.8 copy.53
  (16 shorter events, 0.1 us)
Async XLA Ops:
  7.2 7.8 %copy-start = (bf16[256,128]{1,0:T(8,128)(2,1)S(1)}, bf16[256,128]{1,0:T(8,128)(2,1)}, u32[]{:S(2)}) copy-start(bf16[256,128]{1,0:T(8,128)(2,1)} %param.17) | copy-start | bytes 196612
  7.2 26.6 %all-gather.3.cloned.1.call-start = ((), (), s32[]{:S(2)}) async-start(), calls=%async_computation | async-start | bytes 1331200 | tf_op jit(solution)/shard_map/all_gather | solution.py:32
  36.9 7.8 %copy-start.1 = (bf16[256,1024]{1,0:T(8,128)(2,1)S(1)}, bf16[256,1024]{1,0:T(8,128)(2,1)}, u32[]{:S(2)}) copy-start(bf16[256,1024]{1,0:T(8,128)(2,1)} %residual_ref.1) | copy-start | bytes 1572868
  36.9 7.8 %copy-start.2 = (f32[4096]{0:T(1024)S(1)}, f32[4096]{0:T(1024)}, u32[]{:S(2)}) copy-start(f32[4096]{0:T(1024)} %param.22) | copy-start | bytes 49156
  116.2 1.2 copy-start.3
Sparse Core Ops, SparseCore 0:
  14.2 19.5 all-gather.2

commit v5 on v4

--- a/solution.py
+++ b/solution.py
@@ -15,31 +15,92 @@
 HIGHEST = lax.Precision.HIGHEST
 
 
-def split_3(value):
-    high = lax.reduce_precision(value, 8, 7)
-    middle = lax.reduce_precision(value - high, 8, 7)
-    low = value - high - middle
-    return jnp.stack([high, middle, low], axis=1).astype(jnp.bfloat16)
-
-
-def incoming_state(log_decay, local_state, axis):
-    count, mine = (lax.axis_size(axis), lax.axis_index(axis))
+def chain_kernel(
+    count, chunks, decay_ref, state_ref, incoming_ref, stage_ref, landed_ref, send_sem, recv_sem
+):
+    mine = lax.axis_index("seq")
+    last = count - 1
+    heads = state_ref.shape[0] // chunks
+    barrier = pltpu.get_barrier_semaphore()
+
+    def greet(neighbour):
+        pl.semaphore_signal(
+            barrier, inc=1, device_id={"seq": neighbour}, device_id_type=pl.DeviceIdType.MESH
+        )
+
+    @pl.when(mine > 0)
+    def _():
+        greet(mine - 1)
+
+    @pl.when(mine < last)
+    def _():
+        greet(mine + 1)
+
+    @pl.when((mine == 0) | (mine == last))
+    def _():
+        pl.semaphore_wait(barrier, 1)
+
+    @pl.when((mine > 0) & (mine < last))
+    def _():
+        pl.semaphore_wait(barrier, 2)
+
+    def copy(chunk):
+        return pltpu.make_async_remote_copy(
+            src_ref=stage_ref.at[chunk],
+            dst_ref=landed_ref.at[chunk],
+            send_sem=send_sem.at[chunk],
+            recv_sem=recv_sem.at[chunk],
+            device_id={"seq": mine + 1},
+            device_id_type=pl.DeviceIdType.MESH,
+        )
+
+    for chunk in range(chunks):
+        here = pl.ds(chunk * heads, heads)
+
+        @pl.when(mine == 0)
+        def _():
+            incoming_ref[here] = jnp.zeros((heads,) + state_ref.shape[1:], jnp.float32)
+
+        @pl.when(mine > 0)
+        def _():
+            copy(chunk).wait_recv()
+            incoming_ref[here] = landed_ref[chunk].astype(jnp.float32)
+
+        @pl.when(mine < last)
+        def _():
+            for index in range(heads):
+                head = chunk * heads + index
+                outgoing = decay_ref[head] * incoming_ref[head] + state_ref[head]
+                stage_ref[chunk, index] = outgoing.astype(jnp.bfloat16)
+            copy(chunk).start()
+
+    for chunk in range(chunks):
+
+        @pl.when(mine < last)
+        def _():
+            copy(chunk).wait_send()
+
+
+def incoming_state(block_decay, local_state, count):
     heads, width, states = local_state.shape
-    decay_rows = jnp.pad(split_3(log_decay), ((0, 0), (0, states - 3)))
-    packed = jnp.concatenate(
-        [local_state.astype(jnp.bfloat16).reshape(heads * width, states), decay_rows], axis=0
-    )
-    pieces = lax.all_gather(packed, axis)
-    logs = jnp.sum(pieces[:, heads * width :, :3].astype(jnp.float32), axis=2)
-    order = jnp.arange(count)
-    between = (order[None, :] > order[:, None]) & (order[None, :] < mine)
-    reach = jnp.sum(jnp.where(between[:, :, None], logs[None], 0.0), axis=1)
-    factor = jnp.where((order < mine)[:, None], jnp.exp(reach), 0.0)
-    total = jnp.zeros(local_state.shape, jnp.float32)
-    for position in range(count - 1):
-        piece = pieces[position, : heads * width].reshape(heads, width, states)
-        total += factor[position][:, None, None] * piece.astype(jnp.float32)
-    return total
+    chunks = 4 if heads % 4 == 0 else 1
+    slots = (chunks, heads // chunks, width, states)
+    return pl.pallas_call(
+        functools.partial(chain_kernel, count, chunks),
+        out_shape=jax.ShapeDtypeStruct(local_state.shape, jnp.float32),
+        in_specs=[
+            pl.BlockSpec(memory_space=pltpu.SMEM),
+            pl.BlockSpec(memory_space=pltpu.VMEM),
+        ],
+        out_specs=pl.BlockSpec(memory_space=pltpu.VMEM),
+        scratch_shapes=[
+            pltpu.VMEM(slots, jnp.bfloat16),
+            pltpu.VMEM(slots, jnp.bfloat16),
+            pltpu.SemaphoreType.DMA((chunks,)),
+            pltpu.SemaphoreType.DMA((chunks,)),
+        ],
+        compiler_params=pltpu.CompilerParams(collective_id=1, has_side_effects=True),
+    )(block_decay, local_state)
 
 
 def line_kernel(
@@ -437,7 +498,7 @@
     local_state = jnp.einsum(
         "hs,shp,sn->hpn", tail, inputs, state_in.astype(jnp.float32), precision=HIGHEST
     )
-    incoming = incoming_state(cumlog[:, -1], local_state, "seq")
+    incoming = incoming_state(jnp.exp(cumlog[:, -1]), local_state, lax.axis_size("seq"))
     carried = jnp.einsum("hpn,tn->thp", incoming, state_out.astype(jnp.float32), precision=HIGHEST)
     ssm_out = (within + jnp.exp(cumlog).T[:, :, None] * carried) * live[:, None, None]
     mean_square = jnp.mean(ssm_out * ssm_out, axis=2, keepdims=True)

time: 131 us -> 112 us (0.85)
  waiting for transfers between devices: 14.4 us -> 0 us
  between operations: 14.8 us -> 1.45 us
  Pallas kernels: 77.4 us -> 87.7 us
  other arithmetic: 4.26 us -> 2.52 us
    all_gather x1 -> x0, waiting for transfers between devices: 14.4 us -> none  [incoming_state(): pieces = lax.all_gather(packed, axis)]
    pallas_call x1, Pallas kernels: 71.5 us -> 78.1 us  [line_layer(): pl.pallas_call(functools.partial(line_kernel, count, shards, chunks), out...]
    pallas_call x0 -> x1, Pallas kernels: none -> 3.61 us  [incoming_state(): pl.pallas_call(functools.partial(chain_kernel, count, chunks), out_shape=...]
  transfers between devices with their start and end apart: 1 -> 0, of which waited for: 1 -> 0; matrix products, arithmetic and copies ran while one was open for 4% -> 0% of each run, Pallas kernels for 0% -> 0%
where the time goes in v5:
time: 112 us
  Pallas kernels  87.7 us (78%)
  matrix products  15.1 us (13%)
  local copies, waits for them, and re-layouts  4.92 us (4%)
  other arithmetic  2.52 us (2%)
  between operations  1.45 us (1%)
    pallas_call x1, Pallas kernels, line_layer(): pl.pallas_call(functools.partial(line_kernel, count, shards, chunks), out...  78.1 us
    dot_general x1, matrix products, body(): jnp.dot(normed, out_weight, preferred_element_type=jnp.float32)  7.75 us
    pallas_call x1, Pallas kernels, attention(): pl.pallas_call(functools.partial(attention_kernel, group_size), grid=(kv_...  5.94 us
    pallas_call x1, Pallas kernels, incoming_state(): pl.pallas_call(functools.partial(chain_kernel, count, chunks), out_shape=...  3.61 us
    dot_general x1, matrix products, body(): within = jnp.einsum('hts,shp->thp', mixing, inputs, precision=HIGHEST)  3.39 us
    unnamed x12, local copies, waits for them, and re-layouts  3.28 us
    dot_general x1, matrix products, body(): jnp.einsum('hs,shp,sn->hpn', tail, inputs, state_in.astype(jnp.float32),...  2.29 us

profile of v5, /device:TPU:0, one launch (start us, length us, event | category | flops | bytes accessed | tf_op | source)
XLA Modules:
  0.0 111.7 jit_solution(1863635647196705492)
XLA Ops:
  0.6 0.0 copy-start
  1.3 0.7 neg.8
  2.0 0.1 pad_add_fusion.limits_ref
  2.1 0.8 mul.96
  2.8 0.8 multiply_bitcast_fusion.1
  3.6 0.6 reduce-window.6
  4.2 0.2 slice_reduce_fusion
  4.4 0.1 copy_bitcast_fusion
  4.5 0.2 slice_reduce_fusion.1
  4.6 0.5 exp.19.decay_ref
  5.2 0.1 exponential_bitcast_fusion
  5.3 0.0 copy-done
  5.3 1.0 fusion.28
  6.3 1.2 %copy.20 = bf16[256,1024]{0,1:T(8,128)(2,1)S(1)} copy(bf16[256,1024]{1,0:T(8,128)(2,1)} %param.15) | data formatting | bytes 1048576 | tf_op args[2]
  7.6 2.3 %fusion.19.state_ref = f32[16,64,128]{2,1,0:T(8,128)} fusion(bf16[256,16,64]{0,2,1:T(8,128)(2,1)S(1)} %bitcast.51, f32[256,16]{0,1:T(8,128)S(1)} %get-tuple-element.11, bf16[256,128]{1,0:T(8,128)(2,1)} %param.16), kind=kOutput, calls=%fused_computation.20 | convolution fusion | flops 403177472 | bytes 1130496 | tf_op jit(solution)/shard_map/hs,shp,sn->hpn/dot_general | solution.py:498
  9.9 3.6 %shard_map.140 = f32[16,64,128]{2,1,0:T(8,128)} custom-call(f32[16]{0:T(128)} %exp.19.decay_ref, f32[16,64,128]{2,1,0:T(8,128)} %fusion.19.state_ref), custom_call_target="tpu_custom_call" | custom-call | tf_op jit(solution)/shard_map/pallas_call | solution.py:88
  13.5 0.0 copy-start.4
  13.5 3.4 %fusion.13 = f32[256,16,64]{0,2,1:T(8,128)S(1)} fusion(bf16[256,16,64]{0,2,1:T(8,128)(2,1)S(1)} %bitcast.52, f32[16,256]{1,0:T(8,128)S(1)} %get-tuple-element.9, f32[256,256]{1,0:T(8,128)S(1)} %fusion.28, f32[16,256]{1,0:T(8,128)S(1)} %copy_bitcast_fusion, pred[256,256]{1,0:T(8,128)(4,1)S(1)} %iota_compare_fusion), kind=kOutput, calls=%fused_computation.14 | convolution fusion | flops 810549248 | bytes 1933312 | tf_op jit(solution)/shard_map/hts,shp->thp/dot_general | solution.py:496
  16.9 0.0 copy-done.4
  16.9 0.7 multiply_reduce_fusion
  17.6 0.2 multiply_convert_fusion
  17.8 0.0 copy-start.1
  17.8 0.0 copy-start.2
  17.8 7.8 %fusion.29.partial_ref = f32[256,4096]{1,0:T(8,128)} fusion(bf16[256,1024]{0,1:T(8,128)(2,1)S(1)} %bitcast.50, bf16[1024,4096]{1,0:T(8,128)(2,1)} %param.21), kind=kOutput, calls=%fused_computation.42 | convolution fusion | flops 2147483648 | bytes 13107200 | tf_op jit(solution)/shard_map/dot_general | solution.py:509
  25.6 0.0 copy-done.1
  25.6 0.0 copy-done.2
  25.6 78.1 %shard_map.141 = (bf16[256,1024]{1,0:T(8,128)(2,1)S(1)}, bf16[256,1024]{1,0:T(8,128)(2,1)S(1)}, bf16[1024,512]{1,0:T(8,128)(2,1)}) custom-call(f32[256,4096]{1,0:T(8,128)} %fusion.29.partial_ref, bf16[256,1024]{1,0:T(8,128)(2,1)S(1)} %copy-done.1, f32[1,4096]{1,0:T(1,128)S(1)} %bitcast.49, bf16[4096,1024]{1,0:T(8,128)(2,1)} %query_weight_ref.1, ...), custom_call_target="tpu_custom_call" | custom-call | tf_op jit(solution)/shard_map/pallas_call | solution.py:381
  103.7 0.0 copy-start.3
  103.7 1.2 %copy-done.3 = bf16[1024,512]{1,0:T(8,128)(2,1)S(1)} copy-done((bf16[1024,512]{1,0:T(8,128)(2,1)S(1)}, bf16[1024,512]{1,0:T(8,128)(2,1)}, u32[]{:S(2)}) %copy-start.3) | copy-done | bytes 1048600
  104.9 5.9 %shard_map.142 = bf16[256,1024]{1,0:T(8,128)(2,1)} custom-call(s32[2]{0:T(128)S(1)} %pad_add_fusion.limits_ref, bf16[256,1024]{1,0:T(8,128)(2,1)S(1)} %get-tuple-element.6.query_ref, bf16[1024,512]{1,0:T(8,128)(2,1)S(1)} %copy-done.3, bf16[1024,512]{1,0:T(8,128)(2,1)S(1)} %copy-done.3), custom_call_target="tpu_custom_call" | custom-call | flops 1073741824 | bytes 2097152 | tf_op jit(solution)/shard_map/pallas_call | solution.py:442
  110.9 0.8 copy.32
  (6 shorter events, 0.1 us)
Async XLA Ops:
  0.6 4.7 %copy-start = (bf16[256,128]{1,0:T(8,128)(2,1)S(1)}, bf16[256,128]{1,0:T(8,128)(2,1)}, u32[]{:S(2)}) copy-start(bf16[256,128]{1,0:T(8,128)(2,1)} %param.17) | copy-start | bytes 196612
  13.5 3.4 %copy-start.4 = (f32[16,64,128]{2,1,0:T(8,128)S(1)}, f32[16,64,128]{2,1,0:T(8,128)}, u32[]{:S(2)}) copy-start(f32[16,64,128]{2,1,0:T(8,128)} %shard_map.140) | copy-start | bytes 1572868
  17.8 7.8 %copy-start.1 = (bf16[256,1024]{1,0:T(8,128)(2,1)S(1)}, bf16[256,1024]{1,0:T(8,128)(2,1)}, u32[]{:S(2)}) copy-start(bf16[256,1024]{1,0:T(8,128)(2,1)} %residual_ref.1) | copy-start | bytes 1572868
  17.8 7.8 %copy-start.2 = (f32[4096]{0:T(1024)S(1)}, f32[4096]{0:T(1024)}, u32[]{:S(2)}) copy-start(f32[4096]{0:T(1024)} %param.22) | copy-start | bytes 49156
  103.7 1.2 %copy-start.3 = (bf16[1024,512]{1,0:T(8,128)(2,1)S(1)}, bf16[1024,512]{1,0:T(8,128)(2,1)}, u32[]{:S(2)}) copy-start(bf16[1024,512]{1,0:T(8,128)(2,1)} %get-tuple-element.7.key_ref.value_ref) | copy-start | bytes 3145732

commit v6 on v5

--- a/solution.py
+++ b/solution.py
@@ -107,7 +107,8 @@
     count,
     shards,
     chunks,
-    partial_ref,
+    normed_ref,
+    out_weight_ref,
     residual_ref,
     gain_ref,
     query_weight_ref,
@@ -116,6 +117,8 @@
     layer_ref,
     query_ref,
     key_value_ref,
+    block_weight_ref,
+    partial_ref,
     weight_ref,
     attn_ref,
     shared_ref,
@@ -130,6 +133,7 @@
     shard_send,
     shard_recv,
     weight_sem,
+    block_sem,
 ):
     mine = lax.axis_index("head")
     last = count - 1
@@ -149,8 +153,33 @@
             zip((key_weight_ref, value_weight_ref, query_weight_ref), starts)
         )
     ]
+
+    def ordered(index):
+        return jnp.where(2 * mine < count, last - index, index)
+
+    def block_load(index):
+        columns = pl.ds(pl.multiple_of(ordered(index) * width, 128), width)
+        return pltpu.make_async_copy(
+            out_weight_ref.at[:, columns], block_weight_ref.at[index], block_sem.at[index]
+        )
+
+    for index in range(count):
+        block_load(index).start()
     for load in loads:
         load.start()
+
+    def compute_block(index):
+        block_load(index).wait()
+        tile = min(width, 256)
+
+        @pl.loop(0, width // tile)
+        def _(step):
+            columns = pl.ds(pl.multiple_of(step * tile, 128), tile)
+            partial_ref[ordered(index), :, columns] = jnp.dot(
+                normed_ref[...],
+                block_weight_ref[index, :, columns],
+                preferred_element_type=jnp.float32,
+            )
 
     barrier = pltpu.get_barrier_semaphore()
 
@@ -259,8 +288,7 @@
             query_ref[here, columns] = product(tile + 2)
 
     def own_part(chunk, owner):
-        columns = pl.ds(pl.multiple_of(owner * width, 128), width)
-        return partial_ref[pl.ds(chunk * rows, rows), columns]
+        return partial_ref[owner, pl.ds(chunk * rows, rows)]
 
     def sum_step(chunk, step):
         for way in range(2):
@@ -333,6 +361,9 @@
             attn_ref[here, columns] = (block * scale * gain_ref[:, columns]).astype(jnp.bfloat16)
 
     for tick in range(chunks + 2 * last):
+        for index in range(count) if tick < 3 else ():
+            if min(index, 2) == tick:
+                compute_block(index)
         for chunk in range(chunks):
             stage = tick - chunk
             if 0 <= stage < last:
@@ -370,7 +401,7 @@
     key_value_ref[...] = shared_ref[...]
 
 
-def line_layer(partial_value, residual, norm_gain, weights, count, shards):
+def line_layer(normed, out_weight, residual, norm_gain, weights, count, shards):
     rows, width = residual.shape
     model_width = width * count
     query_width, kv_width = weights[0].shape[1], weights[1].shape[1]
@@ -378,6 +409,7 @@
     piece = rows // chunks
     messages = (2, chunks, count - 1)
     vmem = pl.BlockSpec(memory_space=pltpu.VMEM)
+    hbm = pl.BlockSpec(memory_space=pltpu.HBM)
     return pl.pallas_call(
         functools.partial(line_kernel, count, shards, chunks),
         out_shape=(
@@ -385,9 +417,11 @@
             jax.ShapeDtypeStruct((rows, query_width), jnp.bfloat16),
             jax.ShapeDtypeStruct((shards * rows, 2 * kv_width), jnp.bfloat16),
         ),
-        in_specs=[vmem] * 3 + [pl.BlockSpec(memory_space=pltpu.HBM)] * 3,
+        in_specs=[vmem, hbm, vmem, vmem, hbm, hbm, hbm],
         out_specs=[vmem] * 3,
         scratch_shapes=[
+            pltpu.VMEM((count, out_weight.shape[0], width), jnp.bfloat16),
+            pltpu.VMEM((count, rows, width), jnp.float32),
             pltpu.VMEM((model_width, 2 * kv_width + query_width), jnp.bfloat16),
             pltpu.VMEM((rows, model_width), jnp.bfloat16),
             pltpu.VMEM((shards * rows, 2 * kv_width), jnp.bfloat16),
@@ -402,11 +436,12 @@
             pltpu.SemaphoreType.DMA((chunks, shards)),
             pltpu.SemaphoreType.DMA((chunks, shards)),
             pltpu.SemaphoreType.DMA((3,)),
+            pltpu.SemaphoreType.DMA((count,)),
         ],
         compiler_params=pltpu.CompilerParams(
             collective_id=0, has_side_effects=True, vmem_limit_bytes=52 * 1024 * 1024
         ),
-    )(partial_value, residual, norm_gain.reshape(1, model_width), *weights)
+    )(normed, out_weight, residual, norm_gain.reshape(1, model_width), *weights)
 
 
 def attention_kernel(group_size, limits_ref, query_ref, key_ref, value_ref, out_ref):
@@ -506,9 +541,9 @@
         ssm_out * lax.rsqrt(mean_square + EPSILON) * ssm_gain.reshape(local_heads, head_width)
     ).astype(jnp.bfloat16)
     normed = normed.reshape(rows, local_heads * head_width)
-    partial_value = jnp.dot(normed, out_weight, preferred_element_type=jnp.float32)
     layer_out, queries, key_value = line_layer(
-        partial_value,
+        normed,
+        out_weight,
         residual,
         norm_gain,
         (query_weight, key_weight, value_weight),

time: 112 us -> 105 us (0.938)
  matrix products: 15.1 us -> 7.34 us
    dot_general x1 -> x0, matrix products: 7.75 us -> none  [body(): jnp.dot(normed, out_weight, preferred_element_type=jnp.float32)]
    unnamed x12 -> x10, local copies, waits for them, and re-layouts: 3.28 us -> 3.28 us
where the time goes in v6:
time: 105 us; the launch traced here: 104 us
  Pallas kernels  87.8 us (84%)
  matrix products  7.34 us (7%)
  local copies, waits for them, and re-layouts  5.12 us (5%)
  other arithmetic  2.52 us (2%)
  between operations  1.45 us (1%)
    pallas_call x1, Pallas kernels, line_layer(): pl.pallas_call(functools.partial(line_kernel, count, shards, chunks), out...  78.3 us
    pallas_call x1, Pallas kernels, attention(): pl.pallas_call(functools.partial(attention_kernel, group_size), grid=(kv_...  5.93 us
    pallas_call x1, Pallas kernels, incoming_state(): pl.pallas_call(functools.partial(chain_kernel, count, chunks), out_shape=...  3.61 us
    dot_general x1, matrix products, body(): within = jnp.einsum('hts,shp->thp', mixing, inputs, precision=HIGHEST)  3.38 us
    unnamed x10, local copies, waits for them, and re-layouts  3.28 us
    dot_general x1, matrix products, body(): jnp.einsum('hs,shp,sn->hpn', tail, inputs, state_in.astype(jnp.float32),...  2.29 us

profile of v6, /device:TPU:0, one launch (start us, length us, event | category | flops | bytes accessed | tf_op | source)
XLA Modules:
  0.0 104.2 jit_solution(832662212234175346)
XLA Ops:
  0.6 0.0 copy-start
  1.3 0.7 neg.8
  2.0 0.1 pad_add_fusion.limits_ref
  2.1 0.8 mul.96
  2.8 0.8 multiply_bitcast_fusion.1
  3.6 0.6 reduce-window.6
  4.2 0.2 slice_reduce_fusion
  4.4 0.1 copy_bitcast_fusion
  4.5 0.2 slice_reduce_fusion.1
  4.6 0.5 exp.19.decay_ref
  5.2 0.1 exponential_bitcast_fusion
  5.3 0.0 copy-done
  5.3 1.0 fusion.28
  6.3 1.2 %copy.21 = bf16[256,1024]{0,1:T(8,128)(2,1)S(1)} copy(bf16[256,1024]{1,0:T(8,128)(2,1)} %param.15) | data formatting | bytes 1048576 | tf_op args[2]
  7.6 2.3 %fusion.19.state_ref = f32[16,64,128]{2,1,0:T(8,128)} fusion(bf16[256,16,64]{0,2,1:T(8,128)(2,1)S(1)} %bitcast.49, f32[256,16]{0,1:T(8,128)S(1)} %get-tuple-element.11, bf16[256,128]{1,0:T(8,128)(2,1)} %param.16), kind=kOutput, calls=%fused_computation.20 | convolution fusion | flops 403177472 | bytes 1130496 | tf_op jit(solution)/shard_map/hs,shp,sn->hpn/dot_general | solution.py:533
  9.9 3.6 %shard_map.140 = f32[16,64,128]{2,1,0:T(8,128)} custom-call(f32[16]{0:T(128)} %exp.19.decay_ref, f32[16,64,128]{2,1,0:T(8,128)} %fusion.19.state_ref), custom_call_target="tpu_custom_call" | custom-call | tf_op jit(solution)/shard_map/pallas_call | solution.py:88
  13.5 0.0 copy-start.3
  13.5 3.4 %fusion.13 = f32[256,16,64]{0,2,1:T(8,128)S(1)} fusion(bf16[256,16,64]{0,2,1:T(8,128)(2,1)S(1)} %bitcast.50, f32[16,256]{1,0:T(8,128)S(1)} %get-tuple-element.9, f32[256,256]{1,0:T(8,128)S(1)} %fusion.28, f32[16,256]{1,0:T(8,128)S(1)} %copy_bitcast_fusion, pred[256,256]{1,0:T(8,128)(4,1)S(1)} %iota_compare_fusion), kind=kOutput, calls=%fused_computation.14 | convolution fusion | flops 810549248 | bytes 1933312 | tf_op jit(solution)/shard_map/hts,shp->thp/dot_general | solution.py:531
  16.9 0.0 copy-done.3
  16.9 0.0 copy-start.1
  16.9 0.6 multiply_reduce_fusion
  17.6 0.2 multiply_convert_fusion
  17.8 0.2 copy.22.normed_ref
  18.0 0.0 copy-done.1
  18.0 78.3 %shard_map.141 = (bf16[256,1024]{1,0:T(8,128)(2,1)S(1)}, bf16[256,1024]{1,0:T(8,128)(2,1)S(1)}, bf16[1024,512]{1,0:T(8,128)(2,1)}) custom-call(bf16[256,1024]{1,0:T(8,128)(2,1)S(1)} %copy.22.normed_ref, bf16[1024,4096]{1,0:T(8,128)(2,1)} %out_weight_ref.1, bf16[256,1024]{1,0:T(8,128)(2,1)} %residual_ref.1, f32[1,4096]{1,0:T(1,128)S(1)} %bitcast.47, ...), custom_call_target="tpu_custom_call" | custom-call | tf_op jit(solution)/shard_map/pallas_call | solution.py:413
  96.3 0.0 copy-start.2
  96.3 1.2 %copy-done.2 = bf16[1024,512]{1,0:T(8,128)(2,1)S(1)} copy-done((bf16[1024,512]{1,0:T(8,128)(2,1)S(1)}, bf16[1024,512]{1,0:T(8,128)(2,1)}, u32[]{:S(2)}) %copy-start.2) | copy-done | bytes 1048600
  97.5 5.9 %shard_map.142 = bf16[256,1024]{1,0:T(8,128)(2,1)} custom-call(s32[2]{0:T(128)S(1)} %pad_add_fusion.limits_ref, bf16[256,1024]{1,0:T(8,128)(2,1)S(1)} %get-tuple-element.6.query_ref, bf16[1024,512]{1,0:T(8,128)(2,1)S(1)} %copy-done.2, bf16[1024,512]{1,0:T(8,128)(2,1)S(1)} %copy-done.2), custom_call_target="tpu_custom_call" | custom-call | flops 1073741824 | bytes 2097152 | tf_op jit(solution)/shard_map/pallas_call | solution.py:477
  103.4 0.8 copy.34
  (6 shorter events, 0.1 us)
Async XLA Ops:
  0.6 4.7 %copy-start = (bf16[256,128]{1,0:T(8,128)(2,1)S(1)}, bf16[256,128]{1,0:T(8,128)(2,1)}, u32[]{:S(2)}) copy-start(bf16[256,128]{1,0:T(8,128)(2,1)} %param.17) | copy-start | bytes 196612
  13.5 3.4 %copy-start.3 = (f32[16,64,128]{2,1,0:T(8,128)S(1)}, f32[16,64,128]{2,1,0:T(8,128)}, u32[]{:S(2)}) copy-start(f32[16,64,128]{2,1,0:T(8,128)} %shard_map.140) | copy-start | bytes 1572868
  16.9 1.1 %copy-start.1 = (f32[4096]{0:T(1024)S(1)}, f32[4096]{0:T(1024)}, u32[]{:S(2)}) copy-start(f32[4096]{0:T(1024)} %param.22) | copy-start | bytes 49156
  96.3 1.2 %copy-start.2 = (bf16[1024,512]{1,0:T(8,128)(2,1)S(1)}, bf16[1024,512]{1,0:T(8,128)(2,1)}, u32[]{:S(2)}) copy-start(bf16[1024,512]{1,0:T(8,128)(2,1)} %get-tuple-element.7.key_ref.value_ref) | copy-start | bytes 3145732

commit v7 on v6

--- a/solution.py
+++ b/solution.py
@@ -364,7 +364,7 @@
         for index in range(count) if tick < 3 else ():
             if min(index, 2) == tick:
                 compute_block(index)
-        for chunk in range(chunks):
+        for chunk in reversed(range(chunks)):
             stage = tick - chunk
             if 0 <= stage < last:
                 sum_step(chunk, stage)

time: 105 us -> 107 us (1.019)
  Pallas kernels: 87.8 us -> 90.6 us
    pallas_call x1, Pallas kernels: 78.3 us -> 81 us  [line_layer(): pl.pallas_call(functools.partial(line_kernel, count, shards, chunks), out...]
where the time goes in v7:
time: 107 us
  Pallas kernels  90.6 us (85%)
  matrix products  7.34 us (7%)
  local copies, waits for them, and re-layouts  5.12 us (5%)
  other arithmetic  2.52 us (2%)
  between operations  1.45 us (1%)
    pallas_call x1, Pallas kernels, line_layer(): pl.pallas_call(functools.partial(line_kernel, count, shards, chunks), out...  81 us
    pallas_call x1, Pallas kernels, attention(): pl.pallas_call(functools.partial(attention_kernel, group_size), grid=(kv_...  5.93 us
    pallas_call x1, Pallas kernels, incoming_state(): pl.pallas_call(functools.partial(chain_kernel, count, chunks), out_shape=...  3.61 us
    dot_general x1, matrix products, body(): within = jnp.einsum('hts,shp->thp', mixing, inputs, precision=HIGHEST)  3.38 us
    unnamed x10, local copies, waits for them, and re-layouts  3.28 us
    dot_general x1, matrix products, body(): jnp.einsum('hs,shp,sn->hpn', tail, inputs, state_in.astype(jnp.float32),...  2.29 us

profile of v7, /device:TPU:0, one launch (start us, length us, event | category | flops | bytes accessed | tf_op | source)
XLA Modules:
  0.0 107.0 jit_solution(8497329316941864108)
XLA Ops:
  0.6 0.0 copy-start
  1.3 0.7 neg.8
  2.0 0.1 pad_add_fusion.limits_ref
  2.1 0.8 mul.96
  2.8 0.8 multiply_bitcast_fusion.1
  3.6 0.6 reduce-window.6
  4.2 0.2 slice_reduce_fusion
  4.4 0.1 copy_bitcast_fusion
  4.5 0.2 slice_reduce_fusion.1
  4.6 0.5 exp.19.decay_ref
  5.2 0.1 exponential_bitcast_fusion
  5.3 0.0 copy-done
  5.3 1.0 fusion.28
  6.3 1.2 %copy.21 = bf16[256,1024]{0,1:T(8,128)(2,1)S(1)} copy(bf16[256,1024]{1,0:T(8,128)(2,1)} %param.15) | data formatting | bytes 1048576 | tf_op args[2]
  7.6 2.3 %fusion.19.state_ref = f32[16,64,128]{2,1,0:T(8,128)} fusion(bf16[256,16,64]{0,2,1:T(8,128)(2,1)S(1)} %bitcast.49, f32[256,16]{0,1:T(8,128)S(1)} %get-tuple-element.11, bf16[256,128]{1,0:T(8,128)(2,1)} %param.16), kind=kOutput, calls=%fused_computation.20 | convolution fusion | flops 403177472 | bytes 1130496 | tf_op jit(solution)/shard_map/hs,shp,sn->hpn/dot_general | solution.py:533
  9.9 3.6 %shard_map.140 = f32[16,64,128]{2,1,0:T(8,128)} custom-call(f32[16]{0:T(128)} %exp.19.decay_ref, f32[16,64,128]{2,1,0:T(8,128)} %fusion.19.state_ref), custom_call_target="tpu_custom_call" | custom-call | tf_op jit(solution)/shard_map/pallas_call | solution.py:88
  13.5 0.0 copy-start.3
  13.5 3.4 %fusion.13 = f32[256,16,64]{0,2,1:T(8,128)S(1)} fusion(bf16[256,16,64]{0,2,1:T(8,128)(2,1)S(1)} %bitcast.50, f32[16,256]{1,0:T(8,128)S(1)} %get-tuple-element.9, f32[256,256]{1,0:T(8,128)S(1)} %fusion.28, f32[16,256]{1,0:T(8,128)S(1)} %copy_bitcast_fusion, pred[256,256]{1,0:T(8,128)(4,1)S(1)} %iota_compare_fusion), kind=kOutput, calls=%fused_computation.14 | convolution fusion | flops 810549248 | bytes 1933312 | tf_op jit(solution)/shard_map/hts,shp->thp/dot_general | solution.py:531
  16.9 0.0 copy-done.3
  16.9 0.0 copy-start.1
  16.9 0.6 multiply_reduce_fusion
  17.6 0.2 multiply_convert_fusion
  17.8 0.2 copy.22.normed_ref
  18.0 0.0 copy-done.1
  18.0 81.0 %shard_map.141 = (bf16[256,1024]{1,0:T(8,128)(2,1)S(1)}, bf16[256,1024]{1,0:T(8,128)(2,1)S(1)}, bf16[1024,512]{1,0:T(8,128)(2,1)}) custom-call(bf16[256,1024]{1,0:T(8,128)(2,1)S(1)} %copy.22.normed_ref, bf16[1024,4096]{1,0:T(8,128)(2,1)} %out_weight_ref.1, bf16[256,1024]{1,0:T(8,128)(2,1)} %residual_ref.1, f32[1,4096]{1,0:T(1,128)S(1)} %bitcast.47, ...), custom_call_target="tpu_custom_call" | custom-call | tf_op jit(solution)/shard_map/pallas_call | solution.py:413
  99.0 0.0 copy-start.2
  99.1 1.2 %copy-done.2 = bf16[1024,512]{1,0:T(8,128)(2,1)S(1)} copy-done((bf16[1024,512]{1,0:T(8,128)(2,1)S(1)}, bf16[1024,512]{1,0:T(8,128)(2,1)}, u32[]{:S(2)}) %copy-start.2) | copy-done | bytes 1048600
  100.3 5.9 %shard_map.142 = bf16[256,1024]{1,0:T(8,128)(2,1)} custom-call(s32[2]{0:T(128)S(1)} %pad_add_fusion.limits_ref, bf16[256,1024]{1,0:T(8,128)(2,1)S(1)} %get-tuple-element.6.query_ref, bf16[1024,512]{1,0:T(8,128)(2,1)S(1)} %copy-done.2, bf16[1024,512]{1,0:T(8,128)(2,1)S(1)} %copy-done.2), custom_call_target="tpu_custom_call" | custom-call | flops 1073741824 | bytes 2097152 | tf_op jit(solution)/shard_map/pallas_call | solution.py:477
  106.2 0.8 copy.34
  (6 shorter events, 0.1 us)
Async XLA Ops:
  0.6 4.7 %copy-start = (bf16[256,128]{1,0:T(8,128)(2,1)S(1)}, bf16[256,128]{1,0:T(8,128)(2,1)}, u32[]{:S(2)}) copy-start(bf16[256,128]{1,0:T(8,128)(2,1)} %param.17) | copy-start | bytes 196612
  13.5 3.4 %copy-start.3 = (f32[16,64,128]{2,1,0:T(8,128)S(1)}, f32[16,64,128]{2,1,0:T(8,128)}, u32[]{:S(2)}) copy-start(f32[16,64,128]{2,1,0:T(8,128)} %shard_map.140) | copy-start | bytes 1572868
  16.9 1.1 %copy-start.1 = (f32[4096]{0:T(1024)S(1)}, f32[4096]{0:T(1024)}, u32[]{:S(2)}) copy-start(f32[4096]{0:T(1024)} %param.22) | copy-start | bytes 49156
  99.0 1.2 %copy-start.2 = (bf16[1024,512]{1,0:T(8,128)(2,1)S(1)}, bf16[1024,512]{1,0:T(8,128)(2,1)}, u32[]{:S(2)}) copy-start(bf16[1024,512]{1,0:T(8,128)(2,1)} %get-tuple-element.7.key_ref.value_ref) | copy-start | bytes 3145732
